TPU v7x, 32 devices: a whole 2x2x4 slice. The times are simulated.
32 devices in a mesh: gx: 4 (over y, x), gy: 8 (over z, core).
Axes of the slice: x: 2, y: 2, z: 4, core: 2. Of those that a mesh axis runs over, the one named last changes fastest.
Arguments:
- populations: float32 [19, 128, 64, 256], P(None, 'gx', 'gy'), may hold values from 0.02 to 0.08
- mass: float32 [256, 1024], P('gx', 'gy'), may hold values from 0.2 to 1
- modulus: float32 [256, 1024], P('gx', 'gy'), may hold values from 0.1 to 0.5
- cell_live: int32 [256, 1024], P('gx', 'gy'), may hold values 0 or 1
- stiff_ref: float32 [12, 12], replicated, as said below
- rec_block: int32 [131072], P(('gx', 'gy')), may hold values from 0 to 255
- rec_owner: int32 [131072, 1], P(('gx', 'gy')), may hold values from 0 to 31; in each aligned block of 4096 rows (0 to 4095, 4096 to 8191, ...) at most 256 rows name the same one
- rec_node: int32 [131072], P(('gx', 'gy')), may hold values from 0 to 8191
- rbf_weight: float32 [131072, 256], P(('gx', 'gy')), may hold values from 0 to 2
Outputs:
- populations_next: float32 [19, 128, 64, 256], P(None, 'gx', 'gy')
- displacement: float32 [3, 256, 1024], P(None, 'gx', 'gy')
Inputs may be any that keep to these rules, and one draw needn't show every extreme that they name: `rec_owner`: in the records of one device no owner is named more than 256 times, and every owner is named by some record. `stiff_ref`: symmetric with a positive diagonal that exceeds the sum of magnitudes of each row's other entries.
All inputs are finite; a program needn't handle non-finite values. No bound on the sum of `cell_live` on one device may be relied on, other than what follows from the above.
Results may differ from a plain program's by a relative error of at most 0.0003.
Values sent between devices are 32-bit elements; how exact they have to be, the bound alone decides.
A program may use at most 128 MiB of HBM per device.

v0:
```python
import functools
import math

import jax
import jax.numpy as jnp
from jax import lax
from jax.experimental import pallas as pl
from jax.experimental.pallas import tpu as pltpu
from jax.sharding import PartitionSpec as P

MESH = pl.DeviceIdType.MESH
F32 = jnp.float32
BF16 = jnp.bfloat16
LANES = 128

lattice_dirs = (
    (0, 0, 0),
    (1, 0, 0),
    (-1, 0, 0),
    (0, 1, 0),
    (0, -1, 0),
    (0, 0, 1),
    (0, 0, -1),
    (1, 1, 0),
    (-1, -1, 0),
    (1, -1, 0),
    (-1, 1, 0),
    (1, 0, 1),
    (-1, 0, -1),
    (1, 0, -1),
    (-1, 0, 1),
    (0, 1, 1),
    (0, -1, -1),
    (0, 1, -1),
    (0, -1, 1),
)
lattice_weights = (1.0 / 3.0,) + (1.0 / 18.0,) * 6 + (1.0 / 36.0,) * 12
relax_rate = 1.25
coupling = 0.1

x_up = [q for q in range(19) if lattice_dirs[q][0] == 1]
x_down = [q for q in range(19) if lattice_dirs[q][0] == -1]
y_up = [q for q in range(19) if lattice_dirs[q][1] == 1]
y_down = [q for q in range(19) if lattice_dirs[q][1] == -1]
diagonal = [q for q in range(19) if lattice_dirs[q][0] != 0 and lattice_dirs[q][1] != 0]


def combine_dirs(fields, direction):
    total = None
    for axis_pos in range(3):
        if direction[axis_pos] != 0:
            field = fields[axis_pos]
            if total is None:
                total = field if direction[axis_pos] == 1 else -field
            else:
                total = total + field if direction[axis_pos] == 1 else total - field
    return total


def halves(values):
    high = values.astype(BF16)
    low = (values - high.astype(F32)).astype(BF16)
    return high, low


def iota(shape, dim):
    return lax.broadcasted_iota(jnp.int32, shape, dim)


def dot_nt(left, right):
    return lax.dot_general(left, right, (((1,), (1,)), ((), ())), preferred_element_type=F32)


def dot_nn(left, right):
    return lax.dot_general(left, right, (((1,), (0,)), ((), ())), preferred_element_type=F32)


def collide_kernel(pop_ref, relaxed_ref, moment_ref, xu_ref, xd_ref, yu_ref, yd_ref):
    step = pl.program_id(0)
    last = pl.num_programs(0) - 1
    rows, cols, depth = pop_ref.shape[1:]

    def one(row, carry):
        pops = [pop_ref[q, row] for q in range(19)]
        density = pops[0]
        for q in range(1, 19):
            density = density + pops[q]
        moment = []
        for axis_pos in range(3):
            total = None
            for q in range(19):
                sign = lattice_dirs[q][axis_pos]
                if sign == 1:
                    total = pops[q] if total is None else total + pops[q]
                elif sign == -1:
                    total = -pops[q] if total is None else total - pops[q]
            moment.append(total)
            moment_ref[axis_pos, row] = total
        velocity = [moment[axis_pos] / density for axis_pos in range(3)]
        squared = (
            velocity[0] * velocity[0] + velocity[1] * velocity[1] + velocity[2] * velocity[2]
        )
        rest = 1.0 - 1.5 * squared
        for q in range(19):
            projected = combine_dirs(velocity, lattice_dirs[q])
            bracket = rest
            if projected is not None:
                bracket = rest + projected * (3.0 + 4.5 * projected)
            relaxed = (1.0 - relax_rate) * pops[q] + (
                relax_rate * lattice_weights[q]
            ) * density * bracket
            relaxed_ref[q, row] = relaxed
            if q in y_up:
                yu_ref[y_up.index(q), row] = relaxed[cols - 1 : cols]
            if q in y_down:
                yd_ref[y_down.index(q), row] = relaxed[0:1]
        return carry

    lax.fori_loop(0, rows, one, 0, unroll=2)

    @pl.when(step == 0)
    def _():
        for k, q in enumerate(x_down):
            xd_ref[k] = relaxed_ref[q, 0]

    @pl.when(step == last)
    def _():
        for k, q in enumerate(x_up):
            xu_ref[k] = relaxed_ref[q, rows - 1]


def collide(populations):
    _, nx, ny, nz = populations.shape
    rows = 8
    steps = nx // rows
    return pl.pallas_call(
        collide_kernel,
        grid=(steps,),
        in_specs=[pl.BlockSpec((19, rows, ny, nz), lambda i: (0, i, 0, 0))],
        out_specs=[
            pl.BlockSpec((19, rows, ny, nz), lambda i: (0, i, 0, 0)),
            pl.BlockSpec((3, rows, ny, nz), lambda i: (0, i, 0, 0)),
            pl.BlockSpec((5, ny, nz), lambda i: (0, 0, 0)),
            pl.BlockSpec((5, ny, nz), lambda i: (0, 0, 0)),
            pl.BlockSpec((5, rows, 1, nz), lambda i: (0, i, 0, 0)),
            pl.BlockSpec((5, rows, 1, nz), lambda i: (0, i, 0, 0)),
        ],
        out_shape=[
            jax.ShapeDtypeStruct((19, nx, ny, nz), F32),
            jax.ShapeDtypeStruct((3, nx, ny, nz), F32),
            jax.ShapeDtypeStruct((5, ny, nz), F32),
            jax.ShapeDtypeStruct((5, ny, nz), F32),
            jax.ShapeDtypeStruct((5, nx, 1, nz), F32),
            jax.ShapeDtypeStruct((5, nx, 1, nz), F32),
        ],
        compiler_params=pltpu.CompilerParams(dimension_semantics=("arbitrary",)),
        name="collide",
    )(populations)


def pack_kernel(
    devices, parts, node_cols, mom_ref, w_ref, blk_ref, own_ref, node_ref,
    out_ref, slot_ref, mom_cat, tri, base, acc,
):
    step = pl.program_id(0)
    blocks = mom_ref.shape[0] // 3
    chunk = w_ref.shape[0]

    @pl.when(step == 0)
    def _():
        high, low = halves(mom_ref[...])
        mom_cat[...] = jnp.concatenate([high, low, high], axis=1)
        before = iota((chunk, chunk), 0) <= iota((chunk, chunk), 1)
        tri[...] = before.astype(F32).astype(BF16)
        base[...] = jnp.zeros_like(base)
        acc[...] = jnp.zeros_like(acc)

    w_high, w_low = halves(w_ref[...])
    products = dot_nt(mom_cat[...], jnp.concatenate([w_high, w_high, w_low], axis=1))
    here = iota((blocks, chunk), 0) == blk_ref[...]
    loads = [
        jnp.sum(
            jnp.where(here, products[c * blocks : (c + 1) * blocks], 0.0), axis=0, keepdims=True
        )
        for c in range(3)
    ]
    owners = own_ref[...]
    hits = (iota((devices, chunk), 0) == owners).astype(F32)
    counts = dot_nn(hits.astype(BF16), tri[...])
    slots = jnp.sum(hits * (counts - 1.0 + base[:, 0:1]), axis=0, keepdims=True)
    base[...] = base[...] + counts[:, chunk - 1 : chunk]
    slot_id = slots.astype(jnp.int32)
    slot_ref[...] = slot_id
    part = slot_id // LANES
    place = slot_id - part * LANES
    node = node_ref[...]
    node_row = node // node_cols
    node_high = (node_row * node_cols).astype(F32)
    node_low = (node - node_row * node_cols).astype(F32)
    channel = iota((8, chunk), 0) // parts
    in_part = (iota((8, chunk), 0) - channel * parts) == part
    high_rows = jnp.zeros((8, chunk), F32)
    low_rows = jnp.zeros((8, chunk), F32)
    for c in range(4):
        if c < 3:
            high = loads[c].astype(BF16).astype(F32)
            low = loads[c] - high
        else:
            high, low = node_high, node_low
        high_rows = jnp.where(in_part & (channel == c), high, high_rows)
        low_rows = jnp.where(in_part & (channel == c), low, low_rows)
    mine = (iota((devices * 8, chunk), 0) // 8) == owners

    def spread(rows):
        tiled = jnp.broadcast_to(rows[None], (devices, 8, chunk)).reshape(devices * 8, chunk)
        return jnp.where(mine, tiled, 0.0).astype(BF16)

    slot_hot = (iota((LANES, chunk), 0) == place).astype(F32).astype(BF16)
    acc[...] += dot_nt(
        jnp.concatenate([spread(high_rows), spread(low_rows)], axis=1),
        jnp.concatenate([slot_hot, slot_hot], axis=1),
    )

    @pl.when(step == pl.num_programs(0) - 1)
    def _():
        out_ref[...] = acc[...].reshape(devices, 8, LANES)


def pack_loads(devices, parts, node_cols, moment, weights, blk, own, node):
    records, depth = weights.shape
    chunk = 512
    rows3 = moment.shape[0]
    row_spec = pl.BlockSpec((1, chunk), lambda i: (0, i))
    return pl.pallas_call(
        functools.partial(pack_kernel, devices, parts, node_cols),
        grid=(records // chunk,),
        in_specs=[
            pl.BlockSpec((rows3, depth), lambda i: (0, 0)),
            pl.BlockSpec((chunk, depth), lambda i: (i, 0)),
            row_spec,
            row_spec,
            row_spec,
        ],
        out_specs=[
            pl.BlockSpec((devices, 8, LANES), lambda i: (0, 0, 0)),
            row_spec,
        ],
        out_shape=[
            jax.ShapeDtypeStruct((devices, 8, LANES), F32),
            jax.ShapeDtypeStruct((1, records), jnp.int32),
        ],
        scratch_shapes=[
            pltpu.VMEM((rows3, 3 * depth), BF16),
            pltpu.VMEM((chunk, chunk), BF16),
            pltpu.VMEM((devices, LANES), F32),
            pltpu.VMEM((devices * 8, LANES), F32),
        ],
        compiler_params=pltpu.CompilerParams(dimension_semantics=("arbitrary",)),
        name="pack_loads",
    )(moment, weights, blk, own, node)


def position(grid):
    return lax.axis_index("gx"), lax.axis_index("gy")


def greet_all(grid):
    ix, iy = position(grid)
    devices = grid[0] * grid[1]
    me = ix * grid[1] + iy
    barrier = pltpu.get_barrier_semaphore()

    def signal(j, carry):
        other = lax.rem(me + j, devices)
        pl.semaphore_signal(
            barrier, inc=1, device_id=(lax.div(other, grid[1]), lax.rem(other, grid[1])),
            device_id_type=MESH,
        )
        return carry

    lax.fori_loop(1, devices, signal, 0)
    pl.semaphore_wait(barrier, devices - 1)


def broadcast_copy(grid, j, source, target, send_sem, recv_sem):
    ix, iy = position(grid)
    devices = grid[0] * grid[1]
    me = ix * grid[1] + iy
    other = lax.rem(me + j, devices)
    return pltpu.make_async_remote_copy(
        src_ref=source(other),
        dst_ref=target(me),
        send_sem=send_sem.at[j],
        recv_sem=recv_sem.at[j],
        device_id=(lax.div(other, grid[1]), lax.rem(other, grid[1])),
        device_id_type=MESH,
    )


def to_all(grid, source, target, send_sem, recv_sem, start):
    def body(j, carry):
        copy = broadcast_copy(grid, j, source, target, send_sem, recv_sem)
        if start:
            copy.start()
        else:
            copy.wait()
        return carry

    lax.fori_loop(1, grid[0] * grid[1], body, 0)


def neighbour_copy(grid, dx, dy, source, target, send_sem, recv_sem):
    ix, iy = position(grid)
    return pltpu.make_async_remote_copy(
        src_ref=source,
        dst_ref=target,
        send_sem=send_sem,
        recv_sem=recv_sem,
        device_id=(lax.rem(ix + dx + grid[0], grid[0]), lax.rem(iy + dy + grid[1], grid[1])),
        device_id_type=MESH,
    )


def rim_copies(grid, field, side, strip, send_sem, recv_sem):
    rows = field.shape[1]
    copies = [
        neighbour_copy(grid, 0, 1, field, side.at[0], send_sem.at[0], recv_sem.at[0]),
        neighbour_copy(grid, 0, -1, field, side.at[1], send_sem.at[1], recv_sem.at[1]),
    ]
    for k in range(3):
        dy = 1 - k
        copies.append(
            neighbour_copy(
                grid, 1, dy, field.at[:, pl.ds(rows - 8, 8), :], strip.at[k],
                send_sem.at[2 + k], recv_sem.at[2 + k],
            )
        )
    for k in range(3):
        dy = 1 - k
        copies.append(
            neighbour_copy(
                grid, -1, dy, field.at[:, pl.ds(0, 8), :], strip.at[3 + k],
                send_sem.at[5 + k], recv_sem.at[5 + k],
            )
        )
    return copies


def lines_of(ref, first, count, row, parts):
    return jnp.concatenate(
        [ref[first + d, row + p : row + p + 1] for d in range(count) for p in range(parts)],
        axis=1,
    )


def node_hots(ref, first, count, parts, rows, cols):
    node = lines_of(ref, first, count, 3 * parts, parts).astype(jnp.int32)
    row = node // cols
    col = node - row * cols
    width = count * parts * LANES
    row_hot = iota((rows, width), 0) == row
    col_hot = (iota((cols, width), 0) == col).astype(F32).astype(BF16)
    return row_hot, col_hot


def gather_force(parts, pay, force):
    devices = pay.shape[0]
    rows, cols = force.shape[1:]
    count = math.gcd(devices, 4)

    def one(step, total):
        first = step * count
        row_hot, col_hot = node_hots(pay, first, count, parts, rows, cols)
        highs = []
        lows = []
        for c in range(3):
            value = lines_of(pay, first, count, c * parts, parts)
            high = value.astype(BF16).astype(F32)
            highs.append(jnp.where(row_hot, high, 0.0).astype(BF16))
            lows.append(jnp.where(row_hot, value - high, 0.0).astype(BF16))
        left = jnp.concatenate(
            [jnp.concatenate(highs, axis=0), jnp.concatenate(lows, axis=0)], axis=1
        )
        return total + dot_nt(left, jnp.concatenate([col_hot, col_hot], axis=1))

    total = lax.fori_loop(0, devices // count, one, jnp.zeros((3 * rows, cols), F32))
    for c in range(3):
        force[c] = total[c * rows : (c + 1) * rows]


def pick_moved(parts, disp, pay, out):
    devices = pay.shape[0]
    rows, cols = disp[0].shape
    count = math.gcd(devices, 4)
    high, low = halves(jnp.concatenate(disp, axis=0))
    left = jnp.concatenate([high, low], axis=1)

    def one(step, carry):
        first = step * count
        row_hot, col_hot = node_hots(pay, first, count, parts, rows, cols)
        found = dot_nn(left, jnp.concatenate([col_hot, col_hot], axis=0))
        values = [
            jnp.sum(
                jnp.where(row_hot, found[c * rows : (c + 1) * rows], 0.0), axis=0, keepdims=True
            )
            for c in range(3)
        ]
        for d in range(count):
            pieces = []
            for value in values:
                for p in range(parts):
                    at = (d * parts + p) * LANES
                    pieces.append(value[:, at : at + LANES])
            pieces.append(jnp.zeros((8 - 3 * parts, LANES), F32))
            out[first + d] = jnp.concatenate(pieces, axis=0)
        return carry

    lax.fori_loop(0, devices // count, one, 0)


def with_rim(centre, side, strip, c):
    rows, cols = centre.shape[1:]
    left_half = iota((rows, cols), 1) < cols // 2
    main = jnp.concatenate([centre[c], jnp.where(left_half, side[1, c], side[0, c])], axis=1)
    low = iota((8, cols), 0) < 4
    left_strip = iota((8, cols), 1) < cols // 2
    below = jnp.where(low, strip[4, c], strip[1, c])
    corner = jnp.where(
        low,
        jnp.where(left_strip, strip[5, c], strip[3, c]),
        jnp.where(left_strip, strip[2, c], strip[0, c]),
    )
    return jnp.concatenate([main, jnp.concatenate([below, corner], axis=1)], axis=0)


def couple_kernel(
    grid, parts, stiff, pay, xu, xd, yu, yd, modulus_ref, live_ref, mass_ref,
    disp, back_in, xu_in, xd_in, yu_in, yd_in, corner_in,
    pay_in, back, stat, stat_side, stat_strip, force, side, strip, one_buf, two_buf,
    pay_send, pay_recv, back_send, back_recv, lb_send, lb_recv,
    stat_send, stat_recv, rim_send, rim_recv, one_send, one_recv, two_send, two_recv,
):
    ix, iy = position(grid)
    me = ix * grid[1] + iy
    rows, cols = force.shape[1:]
    full = (rows + 8, 2 * cols)
    stat[0] = modulus_ref[...]
    stat[1] = live_ref[...].astype(F32)
    stat[2] = mass_ref[...]
    greet_all(grid)
    to_all(grid, lambda o: pay.at[o], lambda m: pay_in.at[m], pay_send, pay_recv, True)
    stat_copies = rim_copies(grid, stat, stat_side, stat_strip, stat_send, stat_recv)
    nx = yu.shape[1]
    plan = [
        (1, 0, xu, xu_in),
        (-1, 0, xd, xd_in),
        (0, 1, yu, yu_in),
        (0, -1, yd, yd_in),
    ]
    for k, q in enumerate(diagonal):
        dx, dy, _ = lattice_dirs[q]
        edge = yu.at[y_up.index(q)] if dy == 1 else yd.at[y_down.index(q)]
        plan.append((dx, dy, edge.at[nx - 1 if dx == 1 else 0], corner_in.at[k]))
    lb_copies = [
        neighbour_copy(grid, dx, dy, source, target, lb_send.at[number], lb_recv.at[number])
        for number, (dx, dy, source, target) in enumerate(plan)
    ]
    pay_in[me] = pay[me]
    to_all(grid, lambda o: pay.at[o], lambda m: pay_in.at[m], pay_send, pay_recv, False)
    for copy in stat_copies + lb_copies:
        copy.start()
    gather_force(parts, pay_in, force)
    copies = rim_copies(grid, force, side, strip, rim_send, rim_recv)
    for copy in copies:
        copy.start()

    def back_row(a):
        return pltpu.roll(a, full[0] - 1, 0)

    def back_col(a):
        return pltpu.roll(a, full[1] - 1, 1)

    for copy in stat_copies:
        copy.wait()
    moduli = with_rim(stat, stat_side, stat_strip, 0)
    live = with_rim(stat, stat_side, stat_strip, 1)
    mass = with_rim(stat, stat_side, stat_strip, 2)
    next_row = back_row(moduli)
    scale = live * (moduli + next_row + back_col(moduli) + back_col(next_row)) * 0.25

    def operate(fields):
        down = [back_row(f) for f in fields]
        corners = (
            list(fields) + down + [back_col(f) for f in fields] + [back_col(f) for f in down]
        )
        results = []
        for k in range(12):
            total = stiff[k, 0] * corners[0]
            for l in range(1, 12):
                total = total + stiff[k, l] * corners[l]
            results.append(scale * total)
        images = []
        for c in range(3):
            right = results[6 + c] + pltpu.roll(results[9 + c], 1, 0)
            images.append(
                mass * fields[c]
                + results[c]
                + pltpu.roll(results[3 + c], 1, 0)
                + pltpu.roll(right, 1, 1)
            )
        return images

    def inner(a, b):
        total = a[0][:rows, :cols] * b[0][:rows, :cols]
        for c in range(1, 3):
            total = total + a[c][:rows, :cols] * b[c][:rows, :cols]
        return jnp.sum(jnp.sum(total, axis=0, keepdims=True), axis=1, keepdims=True)

    def sum_over_devices(values, buf, send_sem, recv_sem):
        lane = iota((1, LANES), 1)
        line = jnp.zeros((1, LANES), F32)
        for k, value in enumerate(values):
            line = jnp.where(lane == k, value, line)
        buf[me] = line
        source = lambda o: buf.at[me]
        target = lambda m: buf.at[m]
        to_all(grid, source, target, send_sem, recv_sem, True)
        to_all(grid, source, target, send_sem, recv_sem, False)
        total = jnp.sum(buf[...], axis=0)
        return [total[:, k : k + 1] for k in range(len(values))]

    for copy in copies:
        copy.wait()
    field = [with_rim(force, side, strip, c) for c in range(3)]
    image = operate(field)
    ff, fq = sum_over_devices(
        [inner(field, field), inner(field, image)], one_buf, one_send, one_recv
    )
    first = ff / fq
    residual = [field[c] - first * image[c] for c in range(3)]
    second_image = operate(residual)
    rr, rs, rq = sum_over_devices(
        [inner(residual, residual), inner(residual, second_image), inner(residual, image)],
        two_buf, two_send, two_recv,
    )
    ratio = rr / ff
    second = rr / (rs + 2.0 * ratio * rq + ratio * ratio * fq)
    moved = []
    for c in range(3):
        f = field[c][:rows, :cols]
        moved.append(first * f + second * (residual[c][:rows, :cols] + ratio * f))
        disp[c] = moved[c]
    pick_moved(parts, moved, pay_in, back)
    to_all(grid, lambda o: back.at[o], lambda m: back_in.at[m], back_send, back_recv, True)
    back_in[me] = back[me]
    to_all(grid, lambda o: back.at[o], lambda m: back_in.at[m], back_send, back_recv, False)
    for copy in lb_copies:
        copy.wait()


def couple(grid, parts, stiff, pay, xu, xd, yu, yd, modulus, live, mass):
    devices = grid[0] * grid[1]
    depth = xu.shape[2]
    patch = (3,) + mass.shape
    shapes = [patch, pay.shape, xu.shape, xd.shape, yu.shape, yd.shape, (4, 1, depth)]
    vmem = pl.BlockSpec(memory_space=pltpu.VMEM)
    rim = [pltpu.VMEM((2,) + patch, F32), pltpu.VMEM((6, 3, 8, patch[2]), F32)]
    to_each = pltpu.SemaphoreType.DMA((devices,))
    to_near = pltpu.SemaphoreType.DMA((8,))
    return pl.pallas_call(
        functools.partial(couple_kernel, grid, parts),
        in_specs=[pl.BlockSpec(memory_space=pltpu.SMEM)] + [vmem] * 8,
        out_specs=[vmem] * len(shapes),
        out_shape=[jax.ShapeDtypeStruct(shape, F32) for shape in shapes],
        scratch_shapes=[
            pltpu.VMEM(pay.shape, F32),
            pltpu.VMEM(pay.shape, F32),
            pltpu.VMEM(patch, F32),
            *rim,
            pltpu.VMEM(patch, F32),
            *rim,
            pltpu.VMEM((devices, 1, LANES), F32),
            pltpu.VMEM((devices, 1, LANES), F32),
            to_each, to_each, to_each, to_each, to_near, to_near,
            to_near, to_near, to_near, to_near, to_each, to_each, to_each, to_each,
        ],
        compiler_params=pltpu.CompilerParams(collective_id=0, has_side_effects=True),
        name="couple",
    )(stiff, pay, xu, xd, yu, yd, modulus, live, mass)


def forcing_kernel(parts, back_ref, w_ref, blk_ref, own_ref, slot_ref, out_ref, back_cat):
    step = pl.program_id(0)
    devices = back_ref.shape[0]
    blocks = out_ref.shape[0] // 3
    chunk = w_ref.shape[0]

    @pl.when(step == 0)
    def _():
        high, low = halves(back_ref[...].reshape(devices * 8, LANES))
        back_cat[...] = jnp.concatenate([high, low], axis=1)
        out_ref[...] = jnp.zeros_like(out_ref)

    slot_id = slot_ref[...]
    part = slot_id // LANES
    place = slot_id - part * LANES
    slot_hot = (iota((LANES, chunk), 0) == place).astype(F32).astype(BF16)
    found = dot_nn(back_cat[...], jnp.concatenate([slot_hot, slot_hot], axis=0))
    mine = (iota((devices * 8, chunk), 0) // 8) == own_ref[...]
    lines = jnp.sum(jnp.where(mine, found, 0.0).reshape(devices, 8, chunk), axis=0)
    channel = iota((8, chunk), 0) // parts
    in_part = (iota((8, chunk), 0) - channel * parts) == part
    here = iota((blocks, chunk), 0) == blk_ref[...]
    highs = []
    lows = []
    for c in range(3):
        moved = coupling * jnp.sum(
            jnp.where(in_part & (channel == c), lines, 0.0), axis=0, keepdims=True
        )
        high = moved.astype(BF16).astype(F32)
        highs.append(jnp.where(here, high, 0.0).astype(BF16))
        lows.append(jnp.where(here, moved - high, 0.0).astype(BF16))
    high = jnp.concatenate(highs, axis=0)
    low = jnp.concatenate(lows, axis=0)
    w_high, w_low = halves(w_ref[...])
    out_ref[...] += dot_nn(
        jnp.concatenate([high, low, high], axis=1),
        jnp.concatenate([w_high, w_high, w_low], axis=0),
    )


def forcing_of(parts, blocks, back, weights, blk, own, slot):
    records, depth = weights.shape
    chunk = 1024
    row_spec = pl.BlockSpec((1, chunk), lambda i: (0, i))
    return pl.pallas_call(
        functools.partial(forcing_kernel, parts),
        grid=(records // chunk,),
        in_specs=[
            pl.BlockSpec(back.shape, lambda i: (0, 0, 0)),
            pl.BlockSpec((chunk, depth), lambda i: (i, 0)),
            row_spec,
            row_spec,
            row_spec,
        ],
        out_specs=pl.BlockSpec((3 * blocks, depth), lambda i: (0, 0)),
        out_shape=jax.ShapeDtypeStruct((3 * blocks, depth), F32),
        scratch_shapes=[pltpu.VMEM((back.shape[0] * 8, 2 * LANES), BF16)],
        compiler_params=pltpu.CompilerParams(dimension_semantics=("arbitrary",)),
        name="forcing",
    )(back, weights, blk, own, slot)


def stream_kernel(
    cur, prev_ref, next_ref, forcing, xu, xd, yu, yd, yu_prev, yu_next, yd_prev, yd_next, corner,
    out_ref,
):
    step = pl.program_id(0)
    last = pl.num_programs(0) - 1
    rows, ny, nz = cur.shape[1:]
    fields = [forcing[c] for c in range(3)]

    def shifted(block, before, after, dx):
        if dx == 1:
            return jnp.concatenate([before[None], block[: rows - 1]], axis=0)
        if dx == -1:
            return jnp.concatenate([block[1:], after[None]], axis=0)
        return block

    for q in range(19):
        dx, dy, dz = lattice_dirs[q]
        before = after = None
        if dx == 1:
            before = jnp.where(step == 0, xu[x_up.index(q)], prev_ref[q, 0])
        if dx == -1:
            after = jnp.where(step == last, xd[x_down.index(q)], next_ref[q, 0])
        moved = shifted(cur[q], before, after, dx)
        if dy != 0:
            k = y_up.index(q) if dy == 1 else y_down.index(q)
            edge = (yu if dy == 1 else yd)[k]
            if dx == 1:
                before = (yu_prev if dy == 1 else yd_prev)[k, 0]
                before = jnp.where(step == 0, corner[diagonal.index(q)], before)
            if dx == -1:
                after = (yu_next if dy == 1 else yd_next)[k, 0]
                after = jnp.where(step == last, corner[diagonal.index(q)], after)
            edge = shifted(edge, before, after, dx)
            turned = pltpu.roll(moved, dy % ny, 1)
            at_edge = iota((rows, ny, nz), 1) == (0 if dy == 1 else ny - 1)
            moved = jnp.where(at_edge, jnp.broadcast_to(edge, (rows, ny, nz)), turned)
        if dz != 0:
            moved = pltpu.roll(moved, dz % nz, 2)
        projected = combine_dirs(fields, lattice_dirs[q])
        if projected is not None:
            moved = moved + (3.0 * lattice_weights[q]) * projected
        out_ref[q] = moved


def stream(relaxed, forcing, xu, xd, yu, yd, corner):
    _, nx, ny, nz = relaxed.shape
    rows = 8
    steps = nx // rows
    before = lambda i: (0, (i * rows + nx - 1) % nx, 0, 0)
    after = lambda i: (0, (i * rows + rows) % nx, 0, 0)
    whole3 = lambda i: (0, 0, 0)
    blocked = lambda i: (0, i, 0, 0)
    return pl.pallas_call(
        stream_kernel,
        grid=(steps,),
        in_specs=[
            pl.BlockSpec((19, rows, ny, nz), blocked),
            pl.BlockSpec((19, 1, ny, nz), before),
            pl.BlockSpec((19, 1, ny, nz), after),
            pl.BlockSpec((3, rows, ny, nz), blocked),
            pl.BlockSpec((5, ny, nz), whole3),
            pl.BlockSpec((5, ny, nz), whole3),
            pl.BlockSpec((5, rows, 1, nz), blocked),
            pl.BlockSpec((5, rows, 1, nz), blocked),
            pl.BlockSpec((5, 1, 1, nz), before),
            pl.BlockSpec((5, 1, 1, nz), after),
            pl.BlockSpec((5, 1, 1, nz), before),
            pl.BlockSpec((5, 1, 1, nz), after),
            pl.BlockSpec((4, 1, nz), whole3),
        ],
        out_specs=pl.BlockSpec((19, rows, ny, nz), blocked),
        out_shape=jax.ShapeDtypeStruct((19, nx, ny, nz), F32),
        compiler_params=pltpu.CompilerParams(dimension_semantics=("arbitrary",)),
        name="stream",
    )(relaxed, relaxed, relaxed, forcing, xu, xd, yu, yd, yu, yu, yd, yd, corner)


def per_device(
    grid, populations, mass, modulus, cell_live, stiff_ref, rec_block, rec_owner, rec_node,
    rbf_weight,
):
    devices = grid[0] * grid[1]
    _, nx, ny, nz = populations.shape
    records = rec_block.shape[0]
    rows, cols = mass.shape
    capacity = 2 * records // devices
    parts = -(-capacity // LANES)
    relaxed, moment, xu, xd, yu, yd = collide(populations)
    blk = rec_block.reshape(1, records)
    own = rec_owner.reshape(1, records)
    node = rec_node.reshape(1, records)
    pay, slot = pack_loads(
        devices, parts, cols, moment.reshape(3 * nx * ny, nz), rbf_weight, blk, own, node
    )
    displacement, back, xu, xd, yu, yd, corner = couple(
        grid, parts, stiff_ref, pay, xu, xd, yu, yd, modulus, cell_live, mass
    )
    forcing = forcing_of(parts, nx * ny, back, rbf_weight, blk, own, slot)
    out = stream(relaxed, forcing.reshape(3, nx, ny, nz), xu, xd, yu, yd, corner)
    return out, displacement


def solution(mesh):
    grid = (mesh.shape["gx"], mesh.shape["gy"])
    in_specs = (
        P(None, "gx", "gy", None),
        P("gx", "gy"),
        P("gx", "gy"),
        P("gx", "gy"),
        P(),
        P(("gx", "gy")),
        P(("gx", "gy"), None),
        P(("gx", "gy")),
        P(("gx", "gy"), None),
    )
    out_specs = (P(None, "gx", "gy", None), P(None, "gx", "gy"))
    return jax.shard_map(
        functools.partial(per_device, grid), mesh=mesh, in_specs=in_specs, out_specs=out_specs,
        check_vma=False,
    )
```

profile of v0, /device:TPU:0, one launch (start us, length us, event | category | flops | bytes accessed | tf_op | source)
XLA Modules:
  0.0 82.5 jit_solution(4484112046393690956)
XLA Ops:
  0.6 6.6 %collide.1 = (f32[19,32,8,256]{3,2,1,0:T(8,128)}, f32[3,32,8,256]{3,2,1,0:T(8,128)}, f32[5,8,256]{2,1,0:T(8,128)}, f32[5,8,256]{2,1,0:T(8,128)}, f32[5,32,1,256]{3,2,1,0:T(1,128)}, /*index=5*/f32[5,32,1,256]{3,2,1,0:T(1,128)}) custom-call(f32[19,32,8,256]{3,2,1,0:T(8,128)} %pop_ref.1), custom_call_target="tpu_custom_call" | custom-call | tf_op jit(solution)/shard_map/collide/pallas_call | solution.py:136
  7.2 12.3 %pack_loads.1 = (f32[32,8,128]{2,1,0:T(8,128)}, s32[1,4096]{1,0:T(1,128)}) custom-call(f32[768,256]{1,0:T(8,128)} %bitcast.6, f32[4096,256]{1,0:T(8,128)} %w_ref.3, s32[1,4096]{1,0:T(1,128)} %bitcast.7, s32[1,4096]{1,0:T(1,128)} %bitcast.9, s32[1,4096]{1,0:T(1,128)} %bitcast.11), custom_call_target="tpu_custom_call" | custom-call | tf_op jit(solution)/shard_map/pack_loads/pallas_call | solution.py:234
  19.5 47.3 %couple.1 = (f32[3,64,128]{2,1,0:T(8,128)}, f32[32,8,128]{2,1,0:T(8,128)}, f32[5,8,256]{2,1,0:T(8,128)}, f32[5,8,256]{2,1,0:T(8,128)}, f32[5,32,1,256]{3,2,1,0:T...) custom-call(f32[12,12]{1,0:T(8,128)} %stiff.1, f32[32,8,128]{2,1,0:T(8,128)} %get-tuple-element.19.pay, ...), custom_call_target="tpu_custom_call" | custom-call | tf_op jit(solution)/shard_map/couple/pallas_call | solution.py:570
  66.8 9.0 %forcing.1 = f32[768,256]{1,0:T(8,128)} custom-call(f32[32,8,128]{2,1,0:T(8,128)} %get-tuple-element.24.back_ref, f32[4096,256]{1,0:T(8,128)} %w_ref.3, s32[1,4096]{1,0:T(1,128)} %bitcast.8, s32[1,4096]{1,0:T(1,128)} %bitcast.10, s32[1,4096]{1,0:T(1,128)} %get-tuple-element.25.slot_ref), custom_call_target="tpu_custom_call" | custom-call | tf_op jit(solution)/shard_map/forcing/pallas_call | solution.py:636
  75.9 0.0 copy-start
  75.9 6.0 %stream.1 = f32[19,32,8,256]{3,2,1,0:T(8,128)} custom-call(f32[19,32,8,256]{3,2,1,0:T(8,128)} %get-tuple-element.17.cur.prev_ref.next_ref, f32[19,32,8,256]{3,2,1,0:T(8,128)} %get-tuple-element.17.cur.prev_ref.next_ref, f32[19,32,8,256]{3,2,1,0:T(8,128)} %get-tuple-element.17.cur.prev_ref.next_ref, f32[3,32,8,256]{3,2,1,0:T(8,128)} %bitcast.5, ...), custom_call_target="tpu_custom_call" | custom-call | tf_op jit(solution)/shard_map/stream/pallas_call | solution.py:707
  81.8 0.0 copy-done
  81.9 0.6 copy.12
Async XLA Ops:
  75.9 6.0 %copy-start = (f32[3,64,128]{2,1,0:T(8,128)S(1)}, f32[3,64,128]{2,1,0:T(8,128)}, u32[]{:S(2)}) copy-start(f32[3,64,128]{2,1,0:T(8,128)} %get-tuple-element.35) | copy-start | bytes 294916
where the time goes:
time: 82.8 us; the launch traced here: 82.5 us
  Pallas kernels  81.2 us (98%)
    pallas_call x1, Pallas kernels, couple(): pl.pallas_call(functools.partial(couple_kernel, grid, parts), in_specs=[p...  47.3 us
    pallas_call x1, Pallas kernels, pack_loads(): pl.pallas_call(functools.partial(pack_kernel, devices, parts, node_cols),...  12.3 us
    pallas_call x1, Pallas kernels, forcing_of(): pl.pallas_call(functools.partial(forcing_kernel, parts), grid=(records //...  9.04 us
    pallas_call x1, Pallas kernels, collide(): pl.pallas_call(collide_kernel, grid=(steps,), in_specs=[pl.BlockSpec((19,...  6.56 us
    pallas_call x1, Pallas kernels, stream(): pl.pallas_call(stream_kernel, grid=(steps,), in_specs=[pl.BlockSpec((19,...  5.98 us

commit v1 on v0

--- a/solution.py
+++ b/solution.py
@@ -346,62 +346,76 @@
     return copies
 
 
-def lines_of(ref, first, count, row, parts):
+def lines_of(ref, sources, row, parts):
     return jnp.concatenate(
-        [ref[first + d, row + p : row + p + 1] for d in range(count) for p in range(parts)],
-        axis=1,
-    )
-
-
-def node_hots(ref, first, count, parts, rows, cols):
-    node = lines_of(ref, first, count, 3 * parts, parts).astype(jnp.int32)
-    row = node // cols
-    col = node - row * cols
-    width = count * parts * LANES
-    row_hot = iota((rows, width), 0) == row
-    col_hot = (iota((cols, width), 0) == col).astype(F32).astype(BF16)
+        [ref[source, row + p : row + p + 1] for source in sources for p in range(parts)], axis=1
+    )
+
+
+def sources_of(grid, step, count):
+    ix, iy = position(grid)
+    devices = grid[0] * grid[1]
+    me = ix * grid[1] + iy
+    return [lax.rem(me + devices - lax.rem(step * count + d + 1, devices), devices) for d in range(count)]
+
+
+def node_hots(ref, sources, parts, rows, cols):
+    node = lines_of(ref, sources, 3 * parts, parts).astype(jnp.int32)
+    half = rows // 2 * cols
+    top = node // half
+    rest = node - top * half
+    row = rest // cols
+    col = rest - row * cols + top * cols
+    width = len(sources) * parts * LANES
+    row_hot = iota((rows // 2, width), 0) == row
+    col_hot = (iota((2 * cols, width), 0) == col).astype(F32).astype(BF16)
     return row_hot, col_hot
 
 
-def gather_force(parts, pay, force):
+def gather_force(grid, parts, pay, force, arrived):
     devices = pay.shape[0]
     rows, cols = force.shape[1:]
+    half = rows // 2
     count = math.gcd(devices, 4)
 
     def one(step, total):
-        first = step * count
-        row_hot, col_hot = node_hots(pay, first, count, parts, rows, cols)
+        sources = sources_of(grid, step, count)
+        for d in range(count):
+            arrived(step * count + d + 1)
+        row_hot, col_hot = node_hots(pay, sources, parts, rows, cols)
         highs = []
         lows = []
         for c in range(3):
-            value = lines_of(pay, first, count, c * parts, parts)
+            value = lines_of(pay, sources, c * parts, parts)
             high = value.astype(BF16).astype(F32)
             highs.append(jnp.where(row_hot, high, 0.0).astype(BF16))
             lows.append(jnp.where(row_hot, value - high, 0.0).astype(BF16))
-        left = jnp.concatenate(
-            [jnp.concatenate(highs, axis=0), jnp.concatenate(lows, axis=0)], axis=1
-        )
-        return total + dot_nt(left, jnp.concatenate([col_hot, col_hot], axis=1))
-
-    total = lax.fori_loop(0, devices // count, one, jnp.zeros((3 * rows, cols), F32))
+        return total + dot_nt(jnp.concatenate(highs + lows, axis=0), col_hot)
+
+    total = lax.fori_loop(0, devices // count, one, jnp.zeros((6 * half, 2 * cols), F32))
+    total = total[: 3 * half] + total[3 * half :]
     for c in range(3):
-        force[c] = total[c * rows : (c + 1) * rows]
-
-
-def pick_moved(parts, disp, pay, out):
+        piece = total[c * half : (c + 1) * half]
+        force[c] = jnp.concatenate([piece[:, :cols], piece[:, cols:]], axis=0)
+
+
+def pick_nodes(grid, parts, field, pay, out, ready):
     devices = pay.shape[0]
-    rows, cols = disp[0].shape
+    rows, cols = field[0].shape
+    half = rows // 2
     count = math.gcd(devices, 4)
-    high, low = halves(jnp.concatenate(disp, axis=0))
-    left = jnp.concatenate([high, low], axis=1)
+    wide = [jnp.concatenate([f[:half], f[half:]], axis=1) for f in field]
+    high, low = halves(jnp.concatenate(wide, axis=0))
+    left = jnp.concatenate([high, low], axis=0)
 
     def one(step, carry):
-        first = step * count
-        row_hot, col_hot = node_hots(pay, first, count, parts, rows, cols)
-        found = dot_nn(left, jnp.concatenate([col_hot, col_hot], axis=0))
+        sources = sources_of(grid, step, count)
+        row_hot, col_hot = node_hots(pay, sources, parts, rows, cols)
+        found = dot_nn(left, col_hot)
+        found = found[: 3 * half] + found[3 * half :]
         values = [
             jnp.sum(
-                jnp.where(row_hot, found[c * rows : (c + 1) * rows], 0.0), axis=0, keepdims=True
+                jnp.where(row_hot, found[c * half : (c + 1) * half], 0.0), axis=0, keepdims=True
             )
             for c in range(3)
         ]
@@ -412,7 +426,9 @@
                     at = (d * parts + p) * LANES
                     pieces.append(value[:, at : at + LANES])
             pieces.append(jnp.zeros((8 - 3 * parts, LANES), F32))
-            out[first + d] = jnp.concatenate(pieces, axis=0)
+            out[sources[d]] = jnp.concatenate(pieces, axis=0)
+        for d in range(count):
+            ready(step * count + d + 1)
         return carry
 
     lax.fori_loop(0, devices // count, one, 0)
@@ -435,12 +451,13 @@
 
 def couple_kernel(
     grid, parts, stiff, pay, xu, xd, yu, yd, modulus_ref, live_ref, mass_ref,
-    disp, back_in, xu_in, xd_in, yu_in, yd_in, corner_in,
-    pay_in, back, stat, stat_side, stat_strip, force, side, strip, one_buf, two_buf,
-    pay_send, pay_recv, back_send, back_recv, lb_send, lb_recv,
-    stat_send, stat_recv, rim_send, rim_recv, one_send, one_recv, two_send, two_recv,
+    force_out, image_out, scal_out, back_f_in, back_q_in, xu_in, xd_in, yu_in, yd_in, corner_in,
+    pay_in, back_f, back_q, stat, stat_side, stat_strip, force, side, strip, sums,
+    pay_send, pay_recv, backf_send, backf_recv, backq_send, backq_recv, lb_send, lb_recv,
+    stat_send, stat_recv, rim_send, rim_recv, sum_send, sum_recv,
 ):
     ix, iy = position(grid)
+    devices = grid[0] * grid[1]
     me = ix * grid[1] + iy
     rows, cols = force.shape[1:]
     full = (rows + 8, 2 * cols)
@@ -466,13 +483,54 @@
         for number, (dx, dy, source, target) in enumerate(plan)
     ]
     pay_in[me] = pay[me]
-    to_all(grid, lambda o: pay.at[o], lambda m: pay_in.at[m], pay_send, pay_recv, False)
     for copy in stat_copies + lb_copies:
         copy.start()
-    gather_force(parts, pay_in, force)
+
+    def pay_arrived(j):
+        @pl.when(j < devices)
+        def _():
+            broadcast_copy(
+                grid, j, lambda o: pay.at[o], lambda m: pay_in.at[m], pay_send, pay_recv
+            ).wait()
+
+    gather_force(grid, parts, pay_in, force, pay_arrived)
     copies = rim_copies(grid, force, side, strip, rim_send, rim_recv)
     for copy in copies:
         copy.start()
+
+    def back_copy(j, back, back_in, send_sem, recv_sem):
+        other = lax.rem(me + devices - j, devices)
+        return pltpu.make_async_remote_copy(
+            src_ref=back.at[other],
+            dst_ref=back_in.at[me],
+            send_sem=send_sem.at[j],
+            recv_sem=recv_sem.at[j],
+            device_id=(lax.div(other, grid[1]), lax.rem(other, grid[1])),
+            device_id_type=MESH,
+        )
+
+    def sender(*args):
+        def ready(j):
+            @pl.when(j < devices)
+            def _():
+                back_copy(j, *args).start()
+
+        return ready
+
+    def wait_back(*args):
+        def body(j, carry):
+            back_copy(j, *args).wait()
+            return carry
+
+        lax.fori_loop(1, devices, body, 0)
+
+    f_args = (back_f, back_f_in, backf_send, backf_recv)
+    q_args = (back_q, back_q_in, backq_send, backq_recv)
+    own = [force[c] for c in range(3)]
+    for c in range(3):
+        force_out[c] = own[c]
+    pick_nodes(grid, parts, own, pay_in, back_f, sender(*f_args))
+    back_f_in[me] = back_f[me]
 
     def back_row(a):
         return pltpu.roll(a, full[0] - 1, 0)
@@ -511,49 +569,54 @@
         return images
 
     def inner(a, b):
-        total = a[0][:rows, :cols] * b[0][:rows, :cols]
+        total = a[0] * b[0]
         for c in range(1, 3):
-            total = total + a[c][:rows, :cols] * b[c][:rows, :cols]
+            total = total + a[c] * b[c]
         return jnp.sum(jnp.sum(total, axis=0, keepdims=True), axis=1, keepdims=True)
-
-    def sum_over_devices(values, buf, send_sem, recv_sem):
-        lane = iota((1, LANES), 1)
-        line = jnp.zeros((1, LANES), F32)
-        for k, value in enumerate(values):
-            line = jnp.where(lane == k, value, line)
-        buf[me] = line
-        source = lambda o: buf.at[me]
-        target = lambda m: buf.at[m]
-        to_all(grid, source, target, send_sem, recv_sem, True)
-        to_all(grid, source, target, send_sem, recv_sem, False)
-        total = jnp.sum(buf[...], axis=0)
-        return [total[:, k : k + 1] for k in range(len(values))]
 
     for copy in copies:
         copy.wait()
     field = [with_rim(force, side, strip, c) for c in range(3)]
     image = operate(field)
-    ff, fq = sum_over_devices(
-        [inner(field, field), inner(field, image)], one_buf, one_send, one_recv
-    )
-    first = ff / fq
-    residual = [field[c] - first * image[c] for c in range(3)]
-    second_image = operate(residual)
-    rr, rs, rq = sum_over_devices(
-        [inner(residual, residual), inner(residual, second_image), inner(residual, image)],
-        two_buf, two_send, two_recv,
-    )
-    ratio = rr / ff
-    second = rr / (rs + 2.0 * ratio * rq + ratio * ratio * fq)
-    moved = []
+    second = operate(image)
+    f = [a[:rows, :cols] for a in field]
+    q = [a[:rows, :cols] for a in image]
+    s = [a[:rows, :cols] for a in second]
     for c in range(3):
-        f = field[c][:rows, :cols]
-        moved.append(first * f + second * (residual[c][:rows, :cols] + ratio * f))
-        disp[c] = moved[c]
-    pick_moved(parts, moved, pay_in, back)
-    to_all(grid, lambda o: back.at[o], lambda m: back_in.at[m], back_send, back_recv, True)
-    back_in[me] = back[me]
-    to_all(grid, lambda o: back.at[o], lambda m: back_in.at[m], back_send, back_recv, False)
+        image_out[c] = q[c]
+    ff, fq, qq, qs = inner(f, f), inner(f, q), inner(q, q), inner(q, s)
+    guess = jnp.where(qq > 0.0, fq / jnp.where(qq > 0.0, qq, 1.0), 0.0)
+    r0 = [f[c] - guess * q[c] for c in range(3)]
+    u0 = [q[c] - guess * s[c] for c in range(3)]
+    mine = [ff, fq, qq, qs, guess, inner(r0, r0), inner(r0, q), inner(r0, u0), inner(r0, s), inner(q, u0)]
+    lane = iota((1, LANES), 1)
+    line = jnp.zeros((1, LANES), F32)
+    for k, value in enumerate(mine):
+        line = jnp.where(lane == k, value, line)
+    sums[me] = line
+    to_all(grid, lambda o: sums.at[me], lambda m: sums.at[m], sum_send, sum_recv, True)
+    pick_nodes(grid, parts, q, pay_in, back_q, sender(*q_args))
+    back_q_in[me] = back_q[me]
+    to_all(grid, lambda o: sums.at[me], lambda m: sums.at[m], sum_send, sum_recv, False)
+    every = sums[...].reshape(devices, LANES)
+    ff, fq, qq, qs, guess, r0r0, r0q, r0u0, r0s, qu0 = [every[:, k : k + 1] for k in range(len(mine))]
+
+    def total(value):
+        return jnp.sum(value, axis=0, keepdims=True)
+
+    ff_all, fq_all = total(ff), total(fq)
+    first = ff_all / fq_all
+    off = guess - first
+    rr = total(r0r0 + off * (2.0 * r0q + off * qq))
+    rs = total(r0u0 + off * (r0s + qu0 + off * qs))
+    rq = total(r0q + off * qq)
+    ratio = rr / ff_all
+    step_two = rr / (rs + 2.0 * ratio * rq + ratio * ratio * fq_all)
+    alpha = first + step_two * (1.0 + ratio)
+    beta = -(step_two * first)
+    scal_out[...] = jnp.where(lane == 0, alpha, jnp.where(lane == 1, beta, 0.0))
+    wait_back(*f_args)
+    wait_back(*q_args)
     for copy in lb_copies:
         copy.wait()
 
@@ -562,7 +625,10 @@
     devices = grid[0] * grid[1]
     depth = xu.shape[2]
     patch = (3,) + mass.shape
-    shapes = [patch, pay.shape, xu.shape, xd.shape, yu.shape, yd.shape, (4, 1, depth)]
+    shapes = [
+        patch, patch, (1, LANES), pay.shape, pay.shape, xu.shape, xd.shape, yu.shape, yd.shape,
+        (4, 1, depth),
+    ]
     vmem = pl.BlockSpec(memory_space=pltpu.VMEM)
     rim = [pltpu.VMEM((2,) + patch, F32), pltpu.VMEM((6, 3, 8, patch[2]), F32)]
     to_each = pltpu.SemaphoreType.DMA((devices,))
@@ -575,29 +641,36 @@
         scratch_shapes=[
             pltpu.VMEM(pay.shape, F32),
             pltpu.VMEM(pay.shape, F32),
+            pltpu.VMEM(pay.shape, F32),
             pltpu.VMEM(patch, F32),
             *rim,
             pltpu.VMEM(patch, F32),
             *rim,
             pltpu.VMEM((devices, 1, LANES), F32),
-            pltpu.VMEM((devices, 1, LANES), F32),
-            to_each, to_each, to_each, to_each, to_near, to_near,
-            to_near, to_near, to_near, to_near, to_each, to_each, to_each, to_each,
+            to_each, to_each, to_each, to_each, to_each, to_each, to_near, to_near,
+            to_near, to_near, to_near, to_near, to_each, to_each,
         ],
         compiler_params=pltpu.CompilerParams(collective_id=0, has_side_effects=True),
         name="couple",
     )(stiff, pay, xu, xd, yu, yd, modulus, live, mass)
 
 
-def forcing_kernel(parts, back_ref, w_ref, blk_ref, own_ref, slot_ref, out_ref, back_cat):
+def forcing_kernel(
+    parts, scal, force_ref, image_ref, backf_ref, backq_ref, w_ref, blk_ref, own_ref, slot_ref,
+    out_ref, disp_ref, back_cat,
+):
     step = pl.program_id(0)
-    devices = back_ref.shape[0]
+    devices = backf_ref.shape[0]
     blocks = out_ref.shape[0] // 3
     chunk = w_ref.shape[0]
 
     @pl.when(step == 0)
     def _():
-        high, low = halves(back_ref[...].reshape(devices * 8, LANES))
+        alpha = scal[0, 0]
+        beta = scal[0, 1]
+        disp_ref[...] = alpha * force_ref[...] + beta * image_ref[...]
+        back = alpha * backf_ref[...] + beta * backq_ref[...]
+        high, low = halves(back.reshape(devices * 8, LANES))
         back_cat[...] = jnp.concatenate([high, low], axis=1)
         out_ref[...] = jnp.zeros_like(out_ref)
 
@@ -629,26 +702,37 @@
     )
 
 
-def forcing_of(parts, blocks, back, weights, blk, own, slot):
+def forcing_of(parts, blocks, scal, force, image, back_f, back_q, weights, blk, own, slot):
     records, depth = weights.shape
     chunk = 1024
     row_spec = pl.BlockSpec((1, chunk), lambda i: (0, i))
+    whole3 = lambda i: (0, 0, 0)
     return pl.pallas_call(
         functools.partial(forcing_kernel, parts),
         grid=(records // chunk,),
         in_specs=[
-            pl.BlockSpec(back.shape, lambda i: (0, 0, 0)),
+            pl.BlockSpec(memory_space=pltpu.SMEM),
+            pl.BlockSpec(force.shape, whole3),
+            pl.BlockSpec(force.shape, whole3),
+            pl.BlockSpec(back_f.shape, whole3),
+            pl.BlockSpec(back_f.shape, whole3),
             pl.BlockSpec((chunk, depth), lambda i: (i, 0)),
             row_spec,
             row_spec,
             row_spec,
         ],
-        out_specs=pl.BlockSpec((3 * blocks, depth), lambda i: (0, 0)),
-        out_shape=jax.ShapeDtypeStruct((3 * blocks, depth), F32),
-        scratch_shapes=[pltpu.VMEM((back.shape[0] * 8, 2 * LANES), BF16)],
+        out_specs=[
+            pl.BlockSpec((3 * blocks, depth), lambda i: (0, 0)),
+            pl.BlockSpec(force.shape, whole3),
+        ],
+        out_shape=[
+            jax.ShapeDtypeStruct((3 * blocks, depth), F32),
+            jax.ShapeDtypeStruct(force.shape, F32),
+        ],
+        scratch_shapes=[pltpu.VMEM((back_f.shape[0] * 8, 2 * LANES), BF16)],
         compiler_params=pltpu.CompilerParams(dimension_semantics=("arbitrary",)),
         name="forcing",
-    )(back, weights, blk, own, slot)
+    )(scal, force, image, back_f, back_q, weights, blk, own, slot)
 
 
 def stream_kernel(
@@ -746,10 +830,12 @@
     pay, slot = pack_loads(
         devices, parts, cols, moment.reshape(3 * nx * ny, nz), rbf_weight, blk, own, node
     )
-    displacement, back, xu, xd, yu, yd, corner = couple(
+    force, image, scal, back_f, back_q, xu, xd, yu, yd, corner = couple(
         grid, parts, stiff_ref, pay, xu, xd, yu, yd, modulus, cell_live, mass
     )
-    forcing = forcing_of(parts, nx * ny, back, rbf_weight, blk, own, slot)
+    forcing, displacement = forcing_of(
+        parts, nx * ny, scal, force, image, back_f, back_q, rbf_weight, blk, own, slot
+    )
     out = stream(relaxed, forcing.reshape(3, nx, ny, nz), xu, xd, yu, yd, corner)
     return out, displacement
 

time: 82.8 us -> 71.6 us (0.86)
  Pallas kernels: 81.2 us -> 70.6 us
    pallas_call x1, Pallas kernels: 47.3 us -> 36.5 us  [couple(): pl.pallas_call(functools.partial(couple_kernel, grid, parts), in_specs=[p...]
where the time goes in v1:
time: 71.6 us; the launch traced here: 71.2 us
  Pallas kernels  70.6 us (99%)
    pallas_call x1, Pallas kernels, couple(): pl.pallas_call(functools.partial(couple_kernel, grid, parts), in_specs=[p...  36.5 us
    pallas_call x1, Pallas kernels, pack_loads(): pl.pallas_call(functools.partial(pack_kernel, devices, parts, node_cols),...  12.3 us
    pallas_call x1, Pallas kernels, forcing_of(): pl.pallas_call(functools.partial(forcing_kernel, parts), grid=(records //...  9.24 us
    pallas_call x1, Pallas kernels, collide(): pl.pallas_call(collide_kernel, grid=(steps,), in_specs=[pl.BlockSpec((19,...  6.56 us
    pallas_call x1, Pallas kernels, stream(): pl.pallas_call(stream_kernel, grid=(steps,), in_specs=[pl.BlockSpec((19,...  5.98 us

profile of v1, /device:TPU:0, one launch (start us, length us, event | category | flops | bytes accessed | tf_op | source)
XLA Modules:
  0.0 71.2 jit_solution(6906911537057281143)
XLA Ops:
  0.6 6.6 %collide.1 = (f32[19,32,8,256]{3,2,1,0:T(8,128)}, f32[3,32,8,256]{3,2,1,0:T(8,128)}, f32[5,8,256]{2,1,0:T(8,128)}, f32[5,8,256]{2,1,0:T(8,128)}, f32[5,32,1,256]{3,2,1,0:T(1,128)}, /*index=5*/f32[5,32,1,256]{3,2,1,0:T(1,128)}) custom-call(f32[19,32,8,256]{3,2,1,0:T(8,128)} %pop_ref.1), custom_call_target="tpu_custom_call" | custom-call | tf_op jit(solution)/shard_map/collide/pallas_call | solution.py:136
  7.2 12.3 %pack_loads.1 = (f32[32,8,128]{2,1,0:T(8,128)}, s32[1,4096]{1,0:T(1,128)}) custom-call(f32[768,256]{1,0:T(8,128)} %bitcast.6, f32[4096,256]{1,0:T(8,128)} %w_ref.3, s32[1,4096]{1,0:T(1,128)} %bitcast.7, s32[1,4096]{1,0:T(1,128)} %bitcast.9, s32[1,4096]{1,0:T(1,128)} %bitcast.11), custom_call_target="tpu_custom_call" | custom-call | tf_op jit(solution)/shard_map/pack_loads/pallas_call | solution.py:234
  19.5 36.5 %couple.1 = (f32[3,64,128]{2,1,0:T(8,128)}, f32[3,64,128]{2,1,0:T(8,128)}, f32[1,128]{1,0:T(1,128)}, f32[32,8,128]{2,1,0:T(8,128)}, f32[32,8,128]{2,1,0:T(8,128)...) custom-call(f32[12,12]{1,0:T(8,128)} %stiff.1, ...), custom_call_target="tpu_custom_call" | custom-call | tf_op jit(solution)/shard_map/couple/pallas_call | solution.py:636
  56.0 9.2 %forcing.1 = (f32[768,256]{1,0:T(8,128)}, f32[3,64,128]{2,1,0:T(8,128)}) custom-call(f32[1,128]{1,0:T(1,128)} %get-tuple-element.29.scal, f32[3,64,128]{2,1,0:T(8,128)} %get-tuple-element.30.force_ref, f32[3,64,128]{2,1,0:T(8,128)} %get-tuple-element.31.image_ref, f32[32,8,128]{2,1,0:T(8,128)} %get-tuple-element.32.backf_ref, ...), custom_call_target="tpu_custom_call" | custom-call | tf_op jit(solution)/shard_map/forcing/pallas_call | solution.py:710
  65.3 6.0 %stream.1 = f32[19,32,8,256]{3,2,1,0:T(8,128)} custom-call(f32[19,32,8,256]{3,2,1,0:T(8,128)} %get-tuple-element.22.cur.prev_ref.next_ref, f32[19,32,8,256]{3,2,1,0:T(8,128)} %get-tuple-element.22.cur.prev_ref.next_ref, f32[19,32,8,256]{3,2,1,0:T(8,128)} %get-tuple-element.22.cur.prev_ref.next_ref, f32[3,32,8,256]{3,2,1,0:T(8,128)} %bitcast.5, ...), custom_call_target="tpu_custom_call" | custom-call | tf_op jit(solution)/shard_map/stream/pallas_call | solution.py:791

commit v2 on v1

v2 whole, which is shorter than its diff:
```python
import functools
import math

import jax
import jax.numpy as jnp
from jax import lax
from jax.experimental import pallas as pl
from jax.experimental.pallas import tpu as pltpu
from jax.sharding import PartitionSpec as P

MESH = pl.DeviceIdType.MESH
F32 = jnp.float32
BF16 = jnp.bfloat16
LANES = 128

lattice_dirs = (
    (0, 0, 0),
    (1, 0, 0),
    (-1, 0, 0),
    (0, 1, 0),
    (0, -1, 0),
    (0, 0, 1),
    (0, 0, -1),
    (1, 1, 0),
    (-1, -1, 0),
    (1, -1, 0),
    (-1, 1, 0),
    (1, 0, 1),
    (-1, 0, -1),
    (1, 0, -1),
    (-1, 0, 1),
    (0, 1, 1),
    (0, -1, -1),
    (0, 1, -1),
    (0, -1, 1),
)
lattice_weights = (1.0 / 3.0,) + (1.0 / 18.0,) * 6 + (1.0 / 36.0,) * 12
relax_rate = 1.25
coupling = 0.1

x_up = [q for q in range(19) if lattice_dirs[q][0] == 1]
x_down = [q for q in range(19) if lattice_dirs[q][0] == -1]
y_up = [q for q in range(19) if lattice_dirs[q][1] == 1]
y_down = [q for q in range(19) if lattice_dirs[q][1] == -1]
diagonal = [q for q in range(19) if lattice_dirs[q][0] != 0 and lattice_dirs[q][1] != 0]


def combine_dirs(fields, direction):
    total = None
    for axis_pos in range(3):
        if direction[axis_pos] != 0:
            field = fields[axis_pos]
            if total is None:
                total = field if direction[axis_pos] == 1 else -field
            else:
                total = total + field if direction[axis_pos] == 1 else total - field
    return total


def halves(values):
    high = values.astype(BF16)
    low = (values - high.astype(F32)).astype(BF16)
    return high, low


def iota(shape, dim):
    return lax.broadcasted_iota(jnp.int32, shape, dim)


def dot_nt(left, right):
    return lax.dot_general(left, right, (((1,), (1,)), ((), ())), preferred_element_type=F32)


def dot_nn(left, right):
    return lax.dot_general(left, right, (((1,), (0,)), ((), ())), preferred_element_type=F32)


def position(grid):
    return lax.axis_index("gx"), lax.axis_index("gy")


def greet_all(grid):
    ix, iy = position(grid)
    devices = grid[0] * grid[1]
    me = ix * grid[1] + iy
    barrier = pltpu.get_barrier_semaphore()

    def signal(j, carry):
        other = lax.rem(me + j, devices)
        pl.semaphore_signal(
            barrier, inc=1, device_id=(lax.div(other, grid[1]), lax.rem(other, grid[1])),
            device_id_type=MESH,
        )
        return carry

    lax.fori_loop(1, devices, signal, 0)


def await_all(grid):
    pl.semaphore_wait(pltpu.get_barrier_semaphore(), grid[0] * grid[1] - 1)


def broadcast_copy(grid, j, source, target, send_sem, recv_sem):
    ix, iy = position(grid)
    devices = grid[0] * grid[1]
    me = ix * grid[1] + iy
    other = lax.rem(me + j, devices)
    return pltpu.make_async_remote_copy(
        src_ref=source(other),
        dst_ref=target(me),
        send_sem=send_sem.at[j],
        recv_sem=recv_sem.at[j],
        device_id=(lax.div(other, grid[1]), lax.rem(other, grid[1])),
        device_id_type=MESH,
    )


def to_all(grid, source, target, send_sem, recv_sem, start):
    def body(j, carry):
        copy = broadcast_copy(grid, j, source, target, send_sem, recv_sem)
        if start:
            copy.start()
        else:
            copy.wait()
        return carry

    lax.fori_loop(1, grid[0] * grid[1], body, 0)


def neighbour_copy(grid, dx, dy, source, target, send_sem, recv_sem):
    ix, iy = position(grid)
    return pltpu.make_async_remote_copy(
        src_ref=source,
        dst_ref=target,
        send_sem=send_sem,
        recv_sem=recv_sem,
        device_id=(lax.rem(ix + dx + grid[0], grid[0]), lax.rem(iy + dy + grid[1], grid[1])),
        device_id_type=MESH,
    )


def pack_side(field, side_out):
    rows, cols = field.shape[1:]
    for c in range(3):
        tall = jnp.concatenate([field[c], jnp.zeros((cols - rows, cols), F32)], axis=0).T
        side_out[0, c] = tall[cols - 8 :]
        side_out[1, c] = tall[:8]


def rim_copies(grid, field, side_out, side, strip, send_sem, recv_sem):
    rows = field.shape[1]
    copies = []
    for k in range(3):
        dy = 1 - k
        copies.append(
            neighbour_copy(
                grid, 1, dy, field.at[:, pl.ds(rows - 8, 8), :], strip.at[k],
                send_sem.at[2 + k], recv_sem.at[2 + k],
            )
        )
        copies.append(
            neighbour_copy(
                grid, -1, dy, field.at[:, pl.ds(0, 8), :], strip.at[3 + k],
                send_sem.at[5 + k], recv_sem.at[5 + k],
            )
        )
    copies.append(
        neighbour_copy(grid, 0, 1, side_out.at[0], side.at[0], send_sem.at[0], recv_sem.at[0])
    )
    copies.append(
        neighbour_copy(grid, 0, -1, side_out.at[1], side.at[1], send_sem.at[1], recv_sem.at[1])
    )
    return copies


def with_rim(centre, side, strip, c):
    rows, cols = centre.shape[1:]
    beside = jnp.concatenate([side[1, c], jnp.zeros((cols - 16, cols), F32), side[0, c]], axis=0)
    main = jnp.concatenate([centre[c], beside.T[:rows]], axis=1)
    low = iota((8, cols), 0) < 4
    left_strip = iota((8, cols), 1) < cols // 2
    below = jnp.where(low, strip[4, c], strip[1, c])
    corner = jnp.where(
        low,
        jnp.where(left_strip, strip[5, c], strip[3, c]),
        jnp.where(left_strip, strip[2, c], strip[0, c]),
    )
    return jnp.concatenate([main, jnp.concatenate([below, corner], axis=1)], axis=0)


def find_slots(devices, node_cols, own_ref, node_ref, slot_ref, slot_hot, node_pay):
    records = own_ref.shape[1]
    slots = slot_hot.shape[0]
    span = 2 * LANES
    steps = records // span
    before = (iota((span, span), 0) <= iota((span, span), 1)).astype(F32).astype(BF16)
    hits = [
        iota((devices, span), 0) == own_ref[:, i * span : (i + 1) * span] for i in range(steps)
    ]
    base = jnp.full((devices, span), -1.0, F32)
    routed = None
    for i in range(steps):
        counts = dot_nn(hits[i].astype(F32).astype(BF16), before)
        slot = jnp.sum(jnp.where(hits[i], counts + base, 0.0), axis=0, keepdims=True)
        base = base + jnp.broadcast_to(counts[:, span - 1 :], (devices, span))
        slot = slot.astype(jnp.int32)
        slot_ref[:, i * span : (i + 1) * span] = slot
        hot = (iota((slots, span), 0) == slot).astype(F32).astype(BF16)
        slot_hot[:, i * span : (i + 1) * span] = hot
        node = node_ref[:, i * span : (i + 1) * span]
        row = node // node_cols
        col = (node - row * node_cols).astype(F32)
        left = jnp.concatenate(
            [jnp.where(hits[i], row.astype(F32), 0.0), jnp.where(hits[i], col, 0.0)], axis=0
        )
        part = dot_nt(left.astype(BF16), hot)
        routed = part if routed is None else routed + part
    nodes = routed[:devices] * float(node_cols) + routed[devices:]
    for o in range(devices):
        node_pay[o] = nodes[o : o + 1]


def moments(pop, mom, row):
    for axis_pos in range(3):
        total = None
        for q in range(19):
            sign = lattice_dirs[q][axis_pos]
            if sign == 1:
                total = pop[q, row] if total is None else total + pop[q, row]
            elif sign == -1:
                total = -pop[q, row] if total is None else total - pop[q, row]
        mom[axis_pos, row] = total


def collide_row(pop, mom, read, yu, yd, row):
    rows, cols, depth = read.shape[1:]
    pops = [pop[q, row] for q in range(19)]
    density = pops[0]
    for q in range(1, 19):
        density = density + pops[q]
    inverse = 1.0 / density
    velocity = [mom[axis_pos, row] * inverse for axis_pos in range(3)]
    squared = velocity[0] * velocity[0] + velocity[1] * velocity[1] + velocity[2] * velocity[2]
    rest = 1.0 - 1.5 * squared
    scaled = {w: (relax_rate * w) * density for w in sorted(set(lattice_weights))}
    ups = lax.rem(row + 1, rows)
    downs = lax.rem(row + rows - 1, rows)
    for q in range(19):
        dx, dy, dz = lattice_dirs[q]
        projected = combine_dirs(velocity, lattice_dirs[q])
        bracket = rest
        if projected is not None:
            bracket = rest + projected * (3.0 + 4.5 * projected)
        value = (1.0 - relax_rate) * pops[q] + scaled[lattice_weights[q]] * bracket
        if dz != 0:
            value = pltpu.roll(value, dz % depth, 1)
        if dy != 0:
            value = pltpu.roll(value, dy % cols, 0)
        at = ups if dx == 1 else downs if dx == -1 else row
        read[q, at] = value
        if dy == 1:
            yu[y_up.index(q), at] = value[0:1]
        if dy == -1:
            yd[y_down.index(q), at] = value[cols - 1 : cols]


def mend_edges(read, xu, xd, yu, yd, corner):
    rows, cols, depth = read.shape[1:]
    for k, q in enumerate(x_up):
        read[q, 0] = xu[k]
    for k, q in enumerate(x_down):
        read[q, rows - 1] = xd[k]

    def one(row, carry):
        for k, q in enumerate(y_up):
            read[q, row, 0:1] = yu[k, row]
        for k, q in enumerate(y_down):
            read[q, row, cols - 1 : cols] = yd[k, row]
        return carry

    lax.fori_loop(0, rows, one, 0, unroll=4)
    for k, q in enumerate(diagonal):
        dx, dy, _ = lattice_dirs[q]
        at = 0 if dy == 1 else cols - 1
        read[q, 0 if dx == 1 else rows - 1, at : at + 1] = corner[k]


def sources_of(grid, step, count):
    ix, iy = position(grid)
    devices = grid[0] * grid[1]
    me = ix * grid[1] + iy
    return [
        lax.rem(me + devices - lax.rem(step * count + d + 1, devices), devices)
        for d in range(count)
    ]


def node_parts(node, rows, cols):
    node = node.astype(jnp.int32)
    half = rows // 2 * cols
    top = node // half
    rest = node - top * half
    row = rest // cols
    return row, rest - row * cols + top * cols


def lane_row(ref, source, c, parts):
    return jnp.concatenate(
        [ref[source, p * 3 + c : p * 3 + c + 1] for p in range(parts)], axis=1
    )


def gather_force(grid, parts, node_in, node_hot, pay, force, arrived):
    devices = pay.shape[0]
    rows, cols = force.shape[1:]
    half = rows // 2
    slots = parts * LANES
    count = math.gcd(devices, 4)

    def one(step, total):
        sources = sources_of(grid, step, count)
        for d in range(count):
            arrived(step * count + d + 1)
        for source in sources:
            row, _ = node_parts(node_in[source], rows, cols)
            row_hot = iota((half, slots), 0) == row
            highs = []
            lows = []
            for c in range(3):
                value = lane_row(pay, source, c, parts)
                high = value.astype(BF16).astype(F32)
                highs.append(jnp.where(row_hot, high, 0.0).astype(BF16))
                lows.append(jnp.where(row_hot, value - high, 0.0).astype(BF16))
            total = total + dot_nt(jnp.concatenate(highs + lows, axis=0), node_hot[source])
        return total

    total = lax.fori_loop(0, devices // count, one, jnp.zeros((6 * half, 2 * cols), F32))
    total = total[: 3 * half] + total[3 * half :]
    for c in range(3):
        piece = total[c * half : (c + 1) * half]
        force[c] = jnp.concatenate([piece[:, :cols], piece[:, cols:]], axis=0)


def pick_nodes(grid, parts, field, node_in, node_hot, out, ready):
    devices = out.shape[0]
    rows, cols = field[0].shape
    half = rows // 2
    slots = parts * LANES
    count = math.gcd(devices, 4)
    wide = [jnp.concatenate([f[:half], f[half:]], axis=1) for f in field]
    high, low = halves(jnp.concatenate(wide, axis=0))
    left = jnp.concatenate([high, low], axis=0)

    def one(step, carry):
        sources = sources_of(grid, step, count)
        for source in sources:
            row, _ = node_parts(node_in[source], rows, cols)
            row_hot = iota((half, slots), 0) == row
            found = dot_nn(left, node_hot[source])
            found = found[: 3 * half] + found[3 * half :]
            values = [
                jnp.sum(
                    jnp.where(row_hot, found[c * half : (c + 1) * half], 0.0), axis=0, keepdims=True
                )
                for c in range(3)
            ]
            out[source] = jnp.concatenate(
                [value[:, p * LANES : (p + 1) * LANES] for p in range(parts) for value in values],
                axis=0,
            )
        for d in range(count):
            ready(step * count + d + 1)
        return carry

    lax.fori_loop(0, devices // count, one, 0)


def couple_kernel(
    grid, parts, stiff, pop_hbm, w_hbm, blk_hbm, own_hbm, node_hbm, modulus_ref, live_ref, mass_ref,
    read_out, turned_out, force_out, image_out, scal_out, slot_out, back_f_in, back_q_in,
    pop, mom, mom_cat, w, turned, blk, own, node, slot_hot, read, loads,
    xu_in, xd_in, yu_out, yd_out, yu_in, yd_in, corner_in,
    node_pay, node_in, node_hot, pay, pay_in, back_f, back_q,
    stat, stat_out, stat_side, stat_strip, force, side_out, side, strip, sums,
    pop_sem, w_sem, small_sem, turned_sem, read_sem,
    node_send, node_recv, pay_send, pay_recv, backf_send, backf_recv, backq_send, backq_recv,
    lb_send, lb_recv, stat_send, stat_recv, rim_send, rim_recv, sum_send, sum_recv,
):
    ix, iy = position(grid)
    devices = grid[0] * grid[1]
    me = ix * grid[1] + iy
    rows, cols = force.shape[1:]
    full = (rows + 8, 2 * cols)
    nx, ny, nz = read.shape[1:]
    blocks = nx * ny
    records = w.shape[0]
    slots = parts * LANES
    greet_all(grid)
    small = [
        pltpu.make_async_copy(source, target, small_sem.at[k])
        for k, (source, target) in enumerate([(own_hbm, own), (node_hbm, node), (blk_hbm, blk)])
    ]
    pop_rows = nx // 4
    pop_copies = [
        pltpu.make_async_copy(
            pop_hbm.at[:, pl.ds(k * pop_rows, pop_rows)], pop.at[:, pl.ds(k * pop_rows, pop_rows)],
            pop_sem.at[k],
        )
        for k in range(4)
    ]
    span = 4 * LANES
    steps = records // span

    def w_copy(k):
        at = pl.multiple_of(k * span, span)
        return pltpu.make_async_copy(w_hbm.at[pl.ds(at, span)], w.at[pl.ds(at, span)], w_sem.at[k])

    def turned_copy(k):
        at = pl.multiple_of(k * span, span)
        return pltpu.make_async_copy(
            turned.at[:, pl.ds(at, span)], turned_out.at[:, pl.ds(at, span)], turned_sem.at[k]
        )

    for copy in small + pop_copies:
        copy.start()
    for k in range(steps):
        w_copy(k).start()
    stat[0] = modulus_ref[...]
    stat[1] = live_ref[...].astype(F32)
    stat[2] = mass_ref[...]
    pack_side(stat, stat_out)
    for copy in small:
        copy.wait()
    find_slots(devices, cols, own, node, slot_out, slot_hot, node_pay)
    await_all(grid)
    to_all(
        grid, lambda o: node_pay.at[o], lambda m: node_in.at[m], node_send, node_recv, True
    )
    stat_copies = rim_copies(grid, stat, stat_out, stat_side, stat_strip, stat_send, stat_recv)
    for copy in stat_copies:
        copy.start()
    node_in[me] = node_pay[me]

    for k, copy in enumerate(pop_copies):
        copy.wait()

        def moment_row(row, carry):
            moments(pop, mom, row)
            return carry

        lax.fori_loop(k * pop_rows, (k + 1) * pop_rows, moment_row, 0, unroll=2)
    for c in range(3):
        high, low = halves(mom[c].reshape(blocks, nz).T)
        mom_cat[c * nz : (c + 1) * nz, :blocks] = high
        mom_cat[c * nz : (c + 1) * nz, blocks:] = low

    def load_step(k, carry):
        w_copy(k).wait()
        at = pl.multiple_of(k * span, span)
        hot = (iota((blocks, span), 0) == blk[:, pl.ds(at, span)]).astype(F32).astype(BF16)
        picked = dot_nn(mom_cat[...], jnp.concatenate([hot, hot], axis=0))
        flipped = w[pl.ds(at, span), :].T
        turned[:, pl.ds(at, span)] = flipped
        turned_copy(k).start()
        highs = []
        lows = []
        for c in range(3):
            load = jnp.sum(picked[c * nz : (c + 1) * nz] * flipped, axis=0, keepdims=True)
            high = load.astype(BF16).astype(F32)
            highs.append(high)
            lows.append(load - high)
        loads[:, pl.ds(at, span)] = jnp.concatenate(
            highs + lows + [jnp.zeros((2, span), F32)], axis=0
        )
        return carry

    lax.fori_loop(0, steps, load_step, 0)
    routed = None
    for k in range(steps):
        at = k * span
        owners = own[:, at : at + span]
        value = loads[:, at : at + span]
        spread = jnp.concatenate(
            [jnp.where(owners == o, value, 0.0) for o in range(devices)], axis=0
        ).astype(BF16)
        part = dot_nt(spread, slot_hot[:, at : at + span])
        routed = part if routed is None else routed + part
    for o in range(devices):
        tile = routed[o * 8 : o * 8 + 3] + routed[o * 8 + 3 : o * 8 + 6]
        pay[o] = jnp.concatenate(
            [tile[:, p * LANES : (p + 1) * LANES] for p in range(parts)], axis=0
        )
    to_all(grid, lambda o: pay.at[o], lambda m: pay_in.at[m], pay_send, pay_recv, True)
    pay_in[me] = pay[me]

    def collide_step(row, carry):
        collide_row(pop, mom, read, yu_out, yd_out, row)
        return carry

    lax.fori_loop(0, nx, collide_step, 0)
    plan = []
    for k, q in enumerate(x_up):
        plan.append((1, 0, read.at[q, 0], xu_in.at[k]))
    for k, q in enumerate(x_down):
        plan.append((-1, 0, read.at[q, nx - 1], xd_in.at[k]))
    for k, q in enumerate(diagonal):
        dx, dy, _ = lattice_dirs[q]
        edge = yu_out.at[y_up.index(q)] if dy == 1 else yd_out.at[y_down.index(q)]
        plan.append((dx, dy, edge.at[0 if dx == 1 else nx - 1], corner_in.at[k]))
    plan.append((0, 1, yu_out, yu_in))
    plan.append((0, -1, yd_out, yd_in))
    lb_copies = [
        neighbour_copy(grid, dx, dy, source, target, lb_send.at[number], lb_recv.at[number])
        for number, (dx, dy, source, target) in enumerate(plan)
    ]
    to_all(
        grid, lambda o: node_pay.at[o], lambda m: node_in.at[m], node_send, node_recv, False
    )

    def hot_step(d, carry):
        _, col = node_parts(node_in[d], rows, cols)
        node_hot[d] = (iota((2 * cols, slots), 0) == col).astype(F32).astype(BF16)
        return carry

    lax.fori_loop(0, devices, hot_step, 0, unroll=2)

    def pay_arrived(j):
        @pl.when(j < devices)
        def _():
            broadcast_copy(
                grid, j, lambda o: pay.at[o], lambda m: pay_in.at[m], pay_send, pay_recv
            ).wait()

    gather_force(grid, parts, node_in, node_hot, pay_in, force, pay_arrived)
    pack_side(force, side_out)
    copies = rim_copies(grid, force, side_out, side, strip, rim_send, rim_recv)
    for copy in copies + lb_copies:
        copy.start()

    def back_copy(j, back, back_in, send_sem, recv_sem):
        other = lax.rem(me + devices - j, devices)
        return pltpu.make_async_remote_copy(
            src_ref=back.at[other],
            dst_ref=back_in.at[me],
            send_sem=send_sem.at[j],
            recv_sem=recv_sem.at[j],
            device_id=(lax.div(other, grid[1]), lax.rem(other, grid[1])),
            device_id_type=MESH,
        )

    def sender(*args):
        def ready(j):
            @pl.when(j < devices)
            def _():
                back_copy(j, *args).start()

        return ready

    def wait_back(*args):
        def body(j, carry):
            back_copy(j, *args).wait()
            return carry

        lax.fori_loop(1, devices, body, 0)

    f_args = (back_f, back_f_in, backf_send, backf_recv)
    q_args = (back_q, back_q_in, backq_send, backq_recv)
    held = [force[c] for c in range(3)]
    for c in range(3):
        force_out[c] = held[c]
    pick_nodes(grid, parts, held, node_in, node_hot, back_f, sender(*f_args))
    back_f_in[me] = back_f[me]

    def back_row(a):
        return pltpu.roll(a, full[0] - 1, 0)

    def back_col(a):
        return pltpu.roll(a, full[1] - 1, 1)

    for copy in stat_copies:
        copy.wait()
    moduli = with_rim(stat, stat_side, stat_strip, 0)
    live = with_rim(stat, stat_side, stat_strip, 1)
    mass = with_rim(stat, stat_side, stat_strip, 2)
    next_row = back_row(moduli)
    scale = live * (moduli + next_row + back_col(moduli) + back_col(next_row)) * 0.25

    def operate(fields):
        down = [back_row(f) for f in fields]
        corners = (
            list(fields) + down + [back_col(f) for f in fields] + [back_col(f) for f in down]
        )
        results = []
        for k in range(12):
            total = stiff[k, 0] * corners[0]
            for l in range(1, 12):
                total = total + stiff[k, l] * corners[l]
            results.append(scale * total)
        images = []
        for c in range(3):
            right = results[6 + c] + pltpu.roll(results[9 + c], 1, 0)
            images.append(
                mass * fields[c]
                + results[c]
                + pltpu.roll(results[3 + c], 1, 0)
                + pltpu.roll(right, 1, 1)
            )
        return images

    def inner(a, b):
        total = a[0] * b[0]
        for c in range(1, 3):
            total = total + a[c] * b[c]
        return jnp.sum(jnp.sum(total, axis=0, keepdims=True), axis=1, keepdims=True)

    for copy in copies:
        copy.wait()
    field = [with_rim(force, side, strip, c) for c in range(3)]
    image = operate(field)
    second = operate(image)
    f = [a[:rows, :cols] for a in field]
    q = [a[:rows, :cols] for a in image]
    s = [a[:rows, :cols] for a in second]
    for c in range(3):
        image_out[c] = q[c]
    ff, fq, qq, qs = inner(f, f), inner(f, q), inner(q, q), inner(q, s)
    guess = jnp.where(qq > 0.0, fq / jnp.where(qq > 0.0, qq, 1.0), 0.0)
    r0 = [f[c] - guess * q[c] for c in range(3)]
    u0 = [q[c] - guess * s[c] for c in range(3)]
    mine = [
        ff, fq, qq, qs, guess, inner(r0, r0), inner(r0, q), inner(r0, u0), inner(r0, s), inner(q, u0)
    ]
    lane = iota((1, LANES), 1)
    line = jnp.zeros((1, LANES), F32)
    for k, value in enumerate(mine):
        line = jnp.where(lane == k, value, line)
    sums[me] = line
    to_all(grid, lambda o: sums.at[me], lambda m: sums.at[m], sum_send, sum_recv, True)
    pick_nodes(grid, parts, q, node_in, node_hot, back_q, sender(*q_args))
    back_q_in[me] = back_q[me]

    for copy in lb_copies:
        copy.wait()
    mend_edges(read, xu_in, xd_in, yu_in, yd_in, corner_in)
    read_copies = [
        pltpu.make_async_copy(read.at[k], read_out.at[k], read_sem.at[k]) for k in range(19)
    ]
    for copy in read_copies:
        copy.start()
    to_all(grid, lambda o: sums.at[me], lambda m: sums.at[m], sum_send, sum_recv, False)
    every = sums[...].reshape(devices, LANES)
    ff, fq, qq, qs, guess, r0r0, r0q, r0u0, r0s, qu0 = [
        every[:, k : k + 1] for k in range(len(mine))
    ]

    def total(value):
        return jnp.sum(value, axis=0, keepdims=True)

    ff_all, fq_all = total(ff), total(fq)
    first = ff_all / fq_all
    off = guess - first
    rr = total(r0r0 + off * (2.0 * r0q + off * qq))
    rs = total(r0u0 + off * (r0s + qu0 + off * qs))
    rq = total(r0q + off * qq)
    ratio = rr / ff_all
    step_two = rr / (rs + 2.0 * ratio * rq + ratio * ratio * fq_all)
    alpha = first + step_two * (1.0 + ratio)
    beta = -(step_two * first)
    scal_out[...] = jnp.where(lane == 0, alpha, jnp.where(lane == 1, beta, 0.0))

    def turned_wait(k, carry):
        turned_copy(k).wait()
        return carry

    lax.fori_loop(0, steps, turned_wait, 0)
    for copy in read_copies:
        copy.wait()
    wait_back(*f_args)
    wait_back(*q_args)


def couple(grid, parts, stiff, populations, weights, blk, own, node, modulus, live, mass):
    devices = grid[0] * grid[1]
    _, nx, ny, nz = populations.shape
    records = weights.shape[0]
    patch = (3,) + mass.shape
    slots = parts * LANES
    vmem = pl.BlockSpec(memory_space=pltpu.VMEM)
    hbm = pl.BlockSpec(memory_space=pl.ANY)
    rim = [
        pltpu.VMEM((2, 3, 8, patch[2]), F32),
        pltpu.VMEM((2, 3, 8, patch[2]), F32),
        pltpu.VMEM((6, 3, 8, patch[2]), F32),
    ]
    pay = (devices, 3 * parts, LANES)
    back = jax.ShapeDtypeStruct(pay, F32)
    dma = pltpu.SemaphoreType.DMA
    to_each = dma((devices,))
    to_near = dma((8,))
    lines = pltpu.VMEM((1, records), jnp.int32)
    edges = pltpu.VMEM((5, nx, 1, nz), F32)
    return pl.pallas_call(
        functools.partial(couple_kernel, grid, parts),
        in_specs=[pl.BlockSpec(memory_space=pltpu.SMEM)] + [hbm] * 5 + [vmem] * 3,
        out_specs=[hbm, hbm] + [vmem] * 6,
        out_shape=[
            jax.ShapeDtypeStruct(populations.shape, F32),
            jax.ShapeDtypeStruct((nz, records), F32),
            jax.ShapeDtypeStruct(patch, F32),
            jax.ShapeDtypeStruct(patch, F32),
            jax.ShapeDtypeStruct((1, LANES), F32),
            jax.ShapeDtypeStruct((1, records), jnp.int32),
            back,
            back,
        ],
        scratch_shapes=[
            pltpu.VMEM(populations.shape, F32),
            pltpu.VMEM((3, nx, ny, nz), F32),
            pltpu.VMEM((3 * nz, 2 * nx * ny), BF16),
            pltpu.VMEM(weights.shape, F32),
            pltpu.VMEM((nz, records), F32),
            lines, lines, lines,
            pltpu.VMEM((slots, records), BF16),
            pltpu.VMEM(populations.shape, F32),
            pltpu.VMEM((8, records), F32),
            pltpu.VMEM((5, ny, nz), F32),
            pltpu.VMEM((5, ny, nz), F32),
            edges, edges, edges, edges,
            pltpu.VMEM((4, 1, nz), F32),
            pltpu.VMEM((devices, 1, slots), F32),
            pltpu.VMEM((devices, 1, slots), F32),
            pltpu.VMEM((devices, 2 * patch[2], slots), BF16),
            pltpu.VMEM(pay, F32),
            pltpu.VMEM(pay, F32),
            pltpu.VMEM(pay, F32),
            pltpu.VMEM(pay, F32),
            pltpu.VMEM(patch, F32),
            *rim,
            pltpu.VMEM(patch, F32),
            *rim,
            pltpu.VMEM((devices, 1, LANES), F32),
            dma((4,)), dma((records // (4 * LANES),)), dma((3,)), dma((records // (4 * LANES),)),
            dma((19,)),
            to_each, to_each, to_each, to_each, to_each, to_each, to_each, to_each,
            dma((16,)), dma((16,)), to_near, to_near, to_near, to_near, to_each, to_each,
        ],
        compiler_params=pltpu.CompilerParams(collective_id=0, has_side_effects=True),
        name="couple",
    )(stiff, populations, weights, blk, own, node, modulus, live, mass)


def finish_kernel(
    parts, scal, force_ref, image_ref, backf_ref, backq_ref, blk_ref, own_ref, slot_ref,
    turned_hbm, read_hbm, out_hbm, disp_ref,
    turned, read, out, forcing, moved, turned_sem, read_sem, out_sem,
):
    devices = backf_ref.shape[0]
    depth, records = turned.shape
    _, nx, ny, nz = read.shape
    blocks = nx * ny
    slots = parts * LANES
    span = 4 * LANES
    steps = records // span
    turned_copies = [
        pltpu.make_async_copy(
            turned_hbm.at[:, pl.ds(k * span, span)], turned.at[:, pl.ds(k * span, span)],
            turned_sem.at[k],
        )
        for k in range(steps)
    ]
    stages = [
        [0] + [q for q in range(1, 19) if lattice_dirs[q][1] == 0 and lattice_dirs[q][2] == 0],
        [q for q in range(19) if lattice_dirs[q][1] != 0 and lattice_dirs[q][2] == 0],
        [q for q in range(19) if lattice_dirs[q][2] != 0],
    ]
    order = [q for stage in stages for q in stage]
    read_copies = {
        q: pltpu.make_async_copy(read_hbm.at[q], read.at[q], read_sem.at[q]) for q in order
    }
    for copy in turned_copies:
        copy.start()
    for q in order:
        read_copies[q].start()
    alpha = scal[0, 0]
    beta = scal[0, 1]
    disp_ref[...] = alpha * force_ref[...] + beta * image_ref[...]
    back = alpha * backf_ref[...] + beta * backq_ref[...]
    wide = jnp.concatenate([back[:, p * 3 : p * 3 + 3] for p in range(parts)], axis=2)
    high = wide.astype(BF16).astype(F32)
    left = jnp.concatenate([high, wide - high, jnp.zeros((devices, 2, slots), F32)], axis=1)
    left = left.reshape(devices * 8, slots).astype(BF16)

    def move_step(k, carry):
        at = pl.multiple_of(k * span, span)
        hot = (iota((slots, span), 0) == slot_ref[:, pl.ds(at, span)]).astype(F32).astype(BF16)
        found = dot_nn(left, hot)
        owners = own_ref[:, pl.ds(at, span)]
        lines = jnp.zeros((8, span), F32)
        for o in range(devices):
            lines = lines + jnp.where(owners == o, found[o * 8 : o * 8 + 8], 0.0)
        value = coupling * (lines[:3] + lines[3:6])
        moved[:, pl.ds(at, span)] = jnp.concatenate([value, jnp.zeros((5, span), F32)], axis=0)
        return carry

    lax.fori_loop(0, steps, move_step, 0)
    out_copies = {q: pltpu.make_async_copy(out.at[q], out_hbm.at[q], out_sem.at[q]) for q in order}
    for c in range(3):
        total = None
        for k in range(steps):
            if c == 0:
                turned_copies[k].wait()
            at = k * span
            hot = (iota((blocks, span), 0) == blk_ref[:, at : at + span]).astype(F32).astype(BF16)
            high, low = halves(turned[:, at : at + span] * moved[c : c + 1, at : at + span])
            part = dot_nt(
                jnp.concatenate([hot, hot], axis=1), jnp.concatenate([high, low], axis=1)
            )
            total = part if total is None else total + part
        forcing[c] = total.reshape(nx, ny, nz)
        for q in stages[c]:
            read_copies[q].wait()

            def row_step(row, carry, q=q):
                at = pl.multiple_of(row * 8, 8)
                fields = [forcing[axis_pos, pl.ds(at, 8)] if lattice_dirs[q][axis_pos] else None
                          for axis_pos in range(3)]
                projected = combine_dirs(fields, lattice_dirs[q])
                value = read[q, pl.ds(at, 8)]
                if projected is not None:
                    value = value + (3.0 * lattice_weights[q]) * projected
                out[q, pl.ds(at, 8)] = value
                return carry

            lax.fori_loop(0, nx // 8, row_step, 0)
            out_copies[q].start()
    for q in order:
        out_copies[q].wait()


def finish(parts, scal, force, image, back_f, back_q, blk, own, slot, turned, read):
    vmem = pl.BlockSpec(memory_space=pltpu.VMEM)
    hbm = pl.BlockSpec(memory_space=pl.ANY)
    records = blk.shape[1]
    steps = records // (4 * LANES)
    dma = pltpu.SemaphoreType.DMA
    return pl.pallas_call(
        functools.partial(finish_kernel, parts),
        in_specs=[pl.BlockSpec(memory_space=pltpu.SMEM)] + [vmem] * 7 + [hbm] * 2,
        out_specs=[hbm, vmem],
        out_shape=[
            jax.ShapeDtypeStruct(read.shape, F32),
            jax.ShapeDtypeStruct(force.shape, F32),
        ],
        scratch_shapes=[
            pltpu.VMEM(turned.shape, F32),
            pltpu.VMEM(read.shape, F32),
            pltpu.VMEM(read.shape, F32),
            pltpu.VMEM((3,) + read.shape[1:], F32),
            pltpu.VMEM((8, records), F32),
            dma((steps,)), dma((19,)), dma((19,)),
        ],
        name="finish",
    )(scal, force, image, back_f, back_q, blk, own, slot, turned, read)


def per_device(
    grid, populations, mass, modulus, cell_live, stiff_ref, rec_block, rec_owner, rec_node,
    rbf_weight,
):
    devices = grid[0] * grid[1]
    records = rec_block.shape[0]
    capacity = 2 * records // devices
    parts = -(-capacity // LANES)
    blk = rec_block.reshape(1, records)
    own = rec_owner.reshape(1, records)
    node = rec_node.reshape(1, records)
    read, turned, force, image, scal, slot, back_f, back_q = couple(
        grid, parts, stiff_ref, populations, rbf_weight, blk, own, node, modulus, cell_live, mass
    )
    return finish(parts, scal, force, image, back_f, back_q, blk, own, slot, turned, read)


def solution(mesh):
    grid = (mesh.shape["gx"], mesh.shape["gy"])
    in_specs = (
        P(None, "gx", "gy", None),
        P("gx", "gy"),
        P("gx", "gy"),
        P("gx", "gy"),
        P(),
        P(("gx", "gy")),
        P(("gx", "gy"), None),
        P(("gx", "gy")),
        P(("gx", "gy"), None),
    )
    out_specs = (P(None, "gx", "gy", None), P(None, "gx", "gy"))
    return jax.shard_map(
        functools.partial(per_device, grid), mesh=mesh, in_specs=in_specs, out_specs=out_specs,
        check_vma=False,
    )
```

time: 71.6 us -> 59.4 us (0.83)
  Pallas kernels: 70.6 us -> 58.4 us
    pallas_call x4 -> x1, Pallas kernels: 34.1 us -> 14.1 us  [finish(): pl.pallas_call(functools.partial(finish_kernel, parts), in_specs=[pl.Bloc...]
    pallas_call x1, Pallas kernels: 36.5 us -> 44.3 us  [couple(): pl.pallas_call(functools.partial(couple_kernel, grid, parts), in_specs=[p...]
where the time goes in v2:
time: 59.4 us; the launch traced here: 59.2 us
  Pallas kernels  58.4 us (98%)
  between operations  0.8 us (1%)
    pallas_call x1, Pallas kernels, couple(): pl.pallas_call(functools.partial(couple_kernel, grid, parts), in_specs=[p...  44.3 us
    pallas_call x1, Pallas kernels, finish(): pl.pallas_call(functools.partial(finish_kernel, parts), in_specs=[pl.Bloc...  14.1 us

profile of v2, /device:TPU:0, one launch (start us, length us, event | category | flops | bytes accessed | tf_op | source)
XLA Modules:
  0.0 59.2 jit_solution(3691392905459623318)
XLA Ops:
  0.6 44.3 %couple.1 = (f32[19,32,8,256]{3,2,1,0:T(8,128)}, f32[256,4096]{1,0:T(8,128)}, f32[3,64,128]{2,1,0:T(8,128)}, f32[3,64,128]{2,1,0:T(8,128)}, f32[1,128]{1,0:T(1,1...) custom-call(f32[12,12]{1,0:T(8,128)} %stiff.1, f32[19,32,8,256]{3,2,1,0:T(8,128)} %pop_hbm.1, ...), custom_call_target="tpu_custom_call" | custom-call | tf_op jit(solution)/shard_map/couple/pallas_call | solution.py:702
  44.9 14.1 %finish.1 = (f32[19,32,8,256]{3,2,1,0:T(8,128)}, f32[3,64,128]{2,1,0:T(8,128)}) custom-call(f32[1,128]{1,0:T(1,128)} %get-tuple-element.10.scal, f32[3,64,128]{2,1,0:T(8,128)} %get-tuple-element.11.force_ref, f32[3,64,128]{2,1,0:T(8,128)} %get-tuple-element.12.image_ref, f32[32,6,128]{2,1,0:T(8,128)} %get-tuple-element.13.backf_ref, ...), custom_call_target="tpu_custom_call" | custom-call | tf_op jit(solution)/shard_map/finish/pallas_call | solution.py:846

commit v3 on v2

v3 whole, which is shorter than its diff:
```python
import functools
import math

import jax
import jax.numpy as jnp
from jax import lax
from jax.experimental import pallas as pl
from jax.experimental.pallas import tpu as pltpu
from jax.sharding import PartitionSpec as P

MESH = pl.DeviceIdType.MESH
F32 = jnp.float32
BF16 = jnp.bfloat16
LANES = 128

lattice_dirs = (
    (0, 0, 0),
    (1, 0, 0),
    (-1, 0, 0),
    (0, 1, 0),
    (0, -1, 0),
    (0, 0, 1),
    (0, 0, -1),
    (1, 1, 0),
    (-1, -1, 0),
    (1, -1, 0),
    (-1, 1, 0),
    (1, 0, 1),
    (-1, 0, -1),
    (1, 0, -1),
    (-1, 0, 1),
    (0, 1, 1),
    (0, -1, -1),
    (0, 1, -1),
    (0, -1, 1),
)
lattice_weights = (1.0 / 3.0,) + (1.0 / 18.0,) * 6 + (1.0 / 36.0,) * 12
relax_rate = 1.25
coupling = 0.1

x_up = [q for q in range(19) if lattice_dirs[q][0] == 1]
x_down = [q for q in range(19) if lattice_dirs[q][0] == -1]
y_up = [q for q in range(19) if lattice_dirs[q][1] == 1]
y_down = [q for q in range(19) if lattice_dirs[q][1] == -1]
diagonal = [q for q in range(19) if lattice_dirs[q][0] != 0 and lattice_dirs[q][1] != 0]


def combine_dirs(fields, direction):
    total = None
    for axis_pos in range(3):
        if direction[axis_pos] != 0:
            field = fields[axis_pos]
            if total is None:
                total = field if direction[axis_pos] == 1 else -field
            else:
                total = total + field if direction[axis_pos] == 1 else total - field
    return total


def halves(values):
    high = values.astype(BF16)
    low = (values - high.astype(F32)).astype(BF16)
    return high, low


def iota(shape, dim):
    return lax.broadcasted_iota(jnp.int32, shape, dim)


def dot_nt(left, right):
    return lax.dot_general(left, right, (((1,), (1,)), ((), ())), preferred_element_type=F32)


def dot_nn(left, right):
    return lax.dot_general(left, right, (((1,), (0,)), ((), ())), preferred_element_type=F32)


def position(grid):
    return lax.axis_index("gx"), lax.axis_index("gy")


def greet_all(grid):
    ix, iy = position(grid)
    devices = grid[0] * grid[1]
    me = ix * grid[1] + iy
    barrier = pltpu.get_barrier_semaphore()

    def signal(j, carry):
        other = lax.rem(me + j, devices)
        pl.semaphore_signal(
            barrier, inc=1, device_id=(lax.div(other, grid[1]), lax.rem(other, grid[1])),
            device_id_type=MESH,
        )
        return carry

    lax.fori_loop(1, devices, signal, 0)


def await_all(grid):
    pl.semaphore_wait(pltpu.get_barrier_semaphore(), grid[0] * grid[1] - 1)


def send_all(grid, source, target, send_sem, recv_sem):
    ix, iy = position(grid)
    devices = grid[0] * grid[1]
    me = ix * grid[1] + iy

    def body(j, carry):
        other = lax.rem(me + j, devices)
        pltpu.make_async_remote_copy(
            src_ref=source(other),
            dst_ref=target(me),
            send_sem=send_sem,
            recv_sem=recv_sem(j),
            device_id=(lax.div(other, grid[1]), lax.rem(other, grid[1])),
            device_id_type=MESH,
        ).start()
        return carry

    lax.fori_loop(1, devices, body, 0)


def neighbour_copy(grid, dx, dy, source, target, send_sem, recv_sem):
    ix, iy = position(grid)
    return pltpu.make_async_remote_copy(
        src_ref=source,
        dst_ref=target,
        send_sem=send_sem,
        recv_sem=recv_sem,
        device_id=(lax.rem(ix + dx + grid[0], grid[0]), lax.rem(iy + dy + grid[1], grid[1])),
        device_id_type=MESH,
    )


def pack_side(field, side_out):
    rows, cols = field.shape[1:]
    for c in range(3):
        tall = jnp.concatenate([field[c], jnp.zeros((cols - rows, cols), F32)], axis=0).T
        side_out[0, c] = tall[cols - 8 :]
        side_out[1, c] = tall[:8]


def rim_copies(grid, field, side_out, strip, send_sem, recv_sem):
    rows = field.shape[1]
    copies = []
    for k in range(3):
        dy = 1 - k
        copies.append(
            neighbour_copy(
                grid, 1, dy, field.at[:, pl.ds(rows - 8, 8), :], strip.at[k], send_sem, recv_sem
            )
        )
        copies.append(
            neighbour_copy(
                grid, -1, dy, field.at[:, pl.ds(0, 8), :], strip.at[3 + k], send_sem, recv_sem
            )
        )
    copies.append(neighbour_copy(grid, 0, 1, side_out.at[0], strip.at[6], send_sem, recv_sem))
    copies.append(neighbour_copy(grid, 0, -1, side_out.at[1], strip.at[7], send_sem, recv_sem))
    return copies


def settle(grid, buffer, send_sem, recv_sem):
    copy = neighbour_copy(
        grid, 0, 1, buffer, buffer, recv_sem if send_sem is None else send_sem,
        send_sem if recv_sem is None else recv_sem,
    )
    if send_sem is not None:
        copy.wait_send()
    if recv_sem is not None:
        copy.wait_recv()


def with_rim(centre, strip, c):
    rows, cols = centre.shape[1:]
    beside = jnp.concatenate([strip[7, c], jnp.zeros((cols - 16, cols), F32), strip[6, c]], axis=0)
    main = jnp.concatenate([centre[c], beside.T[:rows]], axis=1)
    low = iota((8, cols), 0) < 4
    left_strip = iota((8, cols), 1) < cols // 2
    below = jnp.where(low, strip[4, c], strip[1, c])
    corner = jnp.where(
        low,
        jnp.where(left_strip, strip[5, c], strip[3, c]),
        jnp.where(left_strip, strip[2, c], strip[0, c]),
    )
    return jnp.concatenate([main, jnp.concatenate([below, corner], axis=1)], axis=0)


def spread_rows(values, count):
    rows = jnp.broadcast_to(values, (16, values.shape[1])).astype(BF16)
    return jnp.concatenate([rows] * (count // 16), axis=0)


def one_hot(count, index):
    index = index.astype(F32)
    ramp = iota((count, index.shape[1]), 0).astype(F32).astype(BF16)
    one = jnp.ones(ramp.shape, BF16)
    return jnp.where(ramp == spread_rows(index, count), one, jnp.zeros(ramp.shape, BF16))


def owner_mask(devices, owners):
    lines = (iota((devices * 8, owners.shape[1]), 0) // 8).astype(F32).astype(BF16)
    return lines == spread_rows(owners.astype(F32), devices * 8)


def find_slots(devices, node_cols, own_ref, node_ref, slot_ref, slot_hot, node_pay):
    records = own_ref.shape[1]
    slots = slot_hot.shape[0]
    span = 2 * LANES
    steps = records // span
    before = (iota((span, span), 0) <= iota((span, span), 1)).astype(F32).astype(BF16)
    base = jnp.full((devices, span), -1.0, F32)
    routed = None
    for i in range(steps):
        hits = one_hot(devices, own_ref[:, i * span : (i + 1) * span])
        counts = dot_nn(hits, before)
        slot = jnp.sum(hits.astype(F32) * (counts + base), axis=0, keepdims=True)
        base = base + jnp.broadcast_to(counts[:, span - 1 :], (devices, span))
        slot_ref[:, i * span : (i + 1) * span] = slot.astype(jnp.int32)
        hot = one_hot(slots, slot)
        slot_hot[:, i * span : (i + 1) * span] = hot
        node = node_ref[:, i * span : (i + 1) * span]
        row = node // node_cols
        col = node - row * node_cols
        left = jnp.concatenate(
            [
                hits * spread_rows(row.astype(F32), devices),
                hits * spread_rows(col.astype(F32), devices),
            ],
            axis=0,
        )
        part = dot_nt(left, hot)
        routed = part if routed is None else routed + part
    nodes = routed[:devices] * float(node_cols) + routed[devices:]
    for o in range(devices):
        node_pay[o] = nodes[o : o + 1]


def moments(pop, mom, row):
    for axis_pos in range(3):
        total = None
        for q in range(19):
            sign = lattice_dirs[q][axis_pos]
            if sign == 1:
                total = pop[q, row] if total is None else total + pop[q, row]
            elif sign == -1:
                total = -pop[q, row] if total is None else total - pop[q, row]
        mom[axis_pos, row] = total


def collide_row(pop, mom, read, yu, yd, row):
    rows, cols, depth = read.shape[1:]
    pops = [pop[q, row] for q in range(19)]
    density = pops[0]
    for q in range(1, 19):
        density = density + pops[q]
    inverse = 1.0 / density
    velocity = [mom[axis_pos, row] * inverse for axis_pos in range(3)]
    squared = velocity[0] * velocity[0] + velocity[1] * velocity[1] + velocity[2] * velocity[2]
    rest = 1.0 - 1.5 * squared
    scaled = {w: (relax_rate * w) * density for w in sorted(set(lattice_weights))}
    ups = lax.rem(row + 1, rows)
    downs = lax.rem(row + rows - 1, rows)
    for q in range(19):
        dx, dy, dz = lattice_dirs[q]
        projected = combine_dirs(velocity, lattice_dirs[q])
        bracket = rest
        if projected is not None:
            bracket = rest + projected * (3.0 + 4.5 * projected)
        value = (1.0 - relax_rate) * pops[q] + scaled[lattice_weights[q]] * bracket
        if dz != 0:
            value = pltpu.roll(value, dz % depth, 1)
        if dy != 0:
            value = pltpu.roll(value, dy % cols, 0)
        at = ups if dx == 1 else downs if dx == -1 else row
        read[q, at] = value
        if dy == 1:
            yu[y_up.index(q), at] = value[0:1]
        if dy == -1:
            yd[y_down.index(q), at] = value[cols - 1 : cols]


def mend_edges(read, xu, xd, yu, yd, corner):
    rows, cols, depth = read.shape[1:]
    for k, q in enumerate(x_up):
        read[q, 0] = xu[k]
    for k, q in enumerate(x_down):
        read[q, rows - 1] = xd[k]

    def one(row, carry):
        for k, q in enumerate(y_up):
            read[q, row, 0:1] = yu[k, row]
        for k, q in enumerate(y_down):
            read[q, row, cols - 1 : cols] = yd[k, row]
        return carry

    lax.fori_loop(0, rows, one, 0, unroll=4)
    for k, q in enumerate(diagonal):
        dx, dy, _ = lattice_dirs[q]
        at = 0 if dy == 1 else cols - 1
        read[q, 0 if dx == 1 else rows - 1, at : at + 1] = corner[k]


def sources_of(grid, step, count):
    ix, iy = position(grid)
    devices = grid[0] * grid[1]
    me = ix * grid[1] + iy
    return [
        lax.rem(me + devices - lax.rem(step * count + d + 1, devices), devices)
        for d in range(count)
    ]


def node_parts(node, rows, cols):
    node = node.astype(jnp.int32)
    half = rows // 2 * cols
    top = node // half
    rest = node - top * half
    row = rest // cols
    return row, rest - row * cols + top * cols


def lane_row(ref, source, c, parts):
    return jnp.concatenate(
        [ref[source, p * 3 + c : p * 3 + c + 1] for p in range(parts)], axis=1
    )


def gather_force(grid, parts, node_in, node_hot, pay, force, arrived):
    ix, iy = position(grid)
    devices = pay.shape[0]
    me = ix * grid[1] + iy
    rows, cols = force.shape[1:]
    half = rows // 2
    count = math.gcd(devices, 8)
    total = None
    for step in range(devices // count):
        arrived(step)
        for d in range(count):
            source = lax.rem(me + devices - (step * count + d), devices)
            row, _ = node_parts(node_in[source], rows, cols)
            row_hot = one_hot(half, row)
            highs = []
            lows = []
            for c in range(3):
                value = lane_row(pay, source, c, parts)
                high = value.astype(BF16).astype(F32)
                highs.append(row_hot * spread_rows(high, half))
                lows.append(row_hot * spread_rows(value - high, half))
            part = dot_nt(jnp.concatenate(highs + lows, axis=0), node_hot[source])
            total = part if total is None else total + part
    total = total[: 3 * half] + total[3 * half :]
    for c in range(3):
        piece = total[c * half : (c + 1) * half]
        force[c] = jnp.concatenate([piece[:, :cols], piece[:, cols:]], axis=0)


def pick_nodes(grid, parts, field, node_in, node_hot, out, ready):
    devices = out.shape[0]
    rows, cols = field[0].shape
    half = rows // 2
    slots = parts * LANES
    count = math.gcd(devices, 8)
    wide = [jnp.concatenate([f[:half], f[half:]], axis=1) for f in field]
    high, low = halves(jnp.concatenate(wide, axis=0))
    left = jnp.concatenate([high, low], axis=0)

    def one(step, carry):
        sources = sources_of(grid, step, count)
        for source in sources:
            row, _ = node_parts(node_in[source], rows, cols)
            row_hot = iota((half, slots), 0) == row
            found = dot_nn(left, node_hot[source])
            found = found[: 3 * half] + found[3 * half :]
            values = [
                jnp.sum(
                    jnp.where(row_hot, found[c * half : (c + 1) * half], 0.0), axis=0, keepdims=True
                )
                for c in range(3)
            ]
            out[source] = jnp.concatenate(
                [value[:, p * LANES : (p + 1) * LANES] for p in range(parts) for value in values],
                axis=0,
            )
        for d in range(count):
            ready(step * count + d + 1)
        return carry

    lax.fori_loop(0, devices // count, one, 0)


def couple_kernel(
    grid, parts, stiff_hbm, pop_hbm, w_hbm, blk_hbm, own_hbm, node_hbm, modulus_hbm, live_hbm, mass_hbm,
    read, turned, force, image_buf, slot, scal_out, back_f_in, back_q_in, blk, own,
    stiff, pop, mom, mom_cat, w, node, slot_hot, loads,
    xu_in, xd_in, yu_out, yd_out, yu_in, yd_in, corner_in,
    node_pay, node_in, node_hot, pay, pay_in, back_f, back_q,
    live_in, stat, stat_out, stat_strip, side_out, strip, sums,
    pop_sem, w_sem, small_sem,
    node_sem, pay_send, pay_recv, backf_sem, backq_sem, lb_send, lb_recv, stat_sem, rim_sem, sum_sem,
):
    ix, iy = position(grid)
    devices = grid[0] * grid[1]
    me = ix * grid[1] + iy
    rows, cols = force.shape[1:]
    full = (rows + 8, 2 * cols)
    nx, ny, nz = read.shape[1:]
    blocks = nx * ny
    records = w.shape[0]
    slots = parts * LANES
    others = pl.ds(0, devices - 1)
    greet_all(grid)
    small = [
        pltpu.make_async_copy(source, target, small_sem.at[k])
        for k, (source, target) in enumerate(
            [
                (own_hbm, own), (node_hbm, node), (blk_hbm, blk), (modulus_hbm, stat.at[0]),
                (mass_hbm, stat.at[2]), (live_hbm, live_in), (stiff_hbm, stiff),
            ]
        )
    ]
    pop_rows = nx // 4
    pop_copies = [
        pltpu.make_async_copy(
            pop_hbm.at[:, pl.ds(k * pop_rows, pop_rows)], pop.at[:, pl.ds(k * pop_rows, pop_rows)],
            pop_sem.at[k],
        )
        for k in range(4)
    ]
    span = 4 * LANES
    steps = records // span

    def w_copy(k):
        at = pl.multiple_of(k * span, span)
        return pltpu.make_async_copy(w_hbm.at[pl.ds(at, span)], w.at[pl.ds(at, span)], w_sem.at[k])

    for copy in small + pop_copies:
        copy.start()
    for k in range(steps):
        w_copy(k).start()
    for copy in small[:3]:
        copy.wait()
    find_slots(devices, cols, own, node, slot, slot_hot, node_pay)

    for k, copy in enumerate(pop_copies):
        copy.wait()

        def moment_row(row, carry):
            moments(pop, mom, row)
            return carry

        lax.fori_loop(k * pop_rows, (k + 1) * pop_rows, moment_row, 0, unroll=2)
    for c in range(3):
        high, low = halves(mom[c].reshape(blocks, nz).T)
        mom_cat[c * nz : (c + 1) * nz, :blocks] = high
        mom_cat[c * nz : (c + 1) * nz, blocks:] = low
    await_all(grid)
    send_all(
        grid, lambda o: node_pay.at[o], lambda m: node_in.at[m], node_sem.at[0],
        lambda j: node_sem.at[1],
    )
    node_in[me] = node_pay[me]

    def load_step(k, carry):
        w_copy(k).wait()
        at = pl.multiple_of(k * span, span)
        hot = one_hot(blocks, blk[:, pl.ds(at, span)])
        picked = dot_nn(mom_cat[...], jnp.concatenate([hot, hot], axis=0))
        flipped = w[pl.ds(at, span), :].T
        turned[:, pl.ds(at, span)] = flipped
        highs = []
        lows = []
        for c in range(3):
            load = jnp.sum(picked[c * nz : (c + 1) * nz] * flipped, axis=0, keepdims=True)
            high = load.astype(BF16).astype(F32)
            highs.append(high)
            lows.append(load - high)
        loads[:, pl.ds(at, span)] = jnp.concatenate(
            highs + lows + [jnp.zeros((2, span), F32)], axis=0
        )
        return carry

    lax.fori_loop(0, steps, load_step, 0)
    routed = None
    for k in range(steps):
        at = k * span
        value = loads[:, at : at + span]
        value = jnp.concatenate([value, value], axis=0).astype(BF16)
        value = jnp.concatenate([value] * (devices // 2), axis=0)
        spread = jnp.where(
            owner_mask(devices, own[:, at : at + span]), value, jnp.zeros(value.shape, BF16)
        )
        part = dot_nt(spread, slot_hot[:, at : at + span])
        routed = part if routed is None else routed + part
    for o in range(devices):
        tile = routed[o * 8 : o * 8 + 3] + routed[o * 8 + 3 : o * 8 + 6]
        pay[o] = jnp.concatenate(
            [tile[:, p * LANES : (p + 1) * LANES] for p in range(parts)], axis=0
        )
    batch = math.gcd(devices, 8)
    send_all(
        grid, lambda o: pay.at[o], lambda m: pay_in.at[m], pay_send.at[0],
        lambda j: pay_recv.at[lax.div(j, batch)],
    )
    pay_in[me] = pay[me]
    for copy in small[3:]:
        copy.wait()
    stat[1] = live_in[...].astype(F32)
    pack_side(stat, stat_out)
    for copy in rim_copies(grid, stat, stat_out, stat_strip, stat_sem.at[0], stat_sem.at[1]):
        copy.start()

    settle(grid, node_in.at[others], node_sem.at[0], node_sem.at[1])

    def hot_step(d, carry):
        _, col = node_parts(node_in[d], rows, cols)
        node_hot[d] = one_hot(2 * cols, col)
        return carry

    lax.fori_loop(0, devices, hot_step, 0, unroll=4)

    def collide_step(row, carry):
        collide_row(pop, mom, read, yu_out, yd_out, row)
        return carry

    lax.fori_loop(0, nx, collide_step, 0, unroll=2)
    lb_copies = []

    def lb_copy(number, dx, dy, source, target):
        lb_copies.append(
            neighbour_copy(grid, dx, dy, source, target, lb_send.at[number], lb_recv.at[number])
        )

    for k, q in enumerate(x_up):
        lb_copy(0, 1, 0, read.at[q, 0], xu_in.at[k])
    for k, q in enumerate(x_down):
        lb_copy(1, -1, 0, read.at[q, nx - 1], xd_in.at[k])
    for k, q in enumerate(diagonal):
        dx, dy, _ = lattice_dirs[q]
        edge = yu_out.at[y_up.index(q)] if dy == 1 else yd_out.at[y_down.index(q)]
        lb_copy(2, dx, dy, edge.at[0 if dx == 1 else nx - 1], corner_in.at[k])
    lb_copy(3, 0, 1, yu_out, yu_in)
    lb_copy(4, 0, -1, yd_out, yd_in)

    def pay_arrived(step):
        got = batch - 1 if step == 0 else batch
        settle(grid, pay_in.at[pl.ds(0, got)], None, pay_recv.at[step])

    gather_force(grid, parts, node_in, node_hot, pay_in, force, pay_arrived)
    pack_side(force, side_out)
    for copy in rim_copies(grid, force, side_out, strip, rim_sem.at[0], rim_sem.at[1]) + lb_copies:
        copy.start()

    def sender(back, back_in, sem):
        def ready(j):
            @pl.when(j < devices)
            def _():
                other = lax.rem(me + devices - j, devices)
                pltpu.make_async_remote_copy(
                    src_ref=back.at[other],
                    dst_ref=back_in.at[me],
                    send_sem=sem.at[0],
                    recv_sem=sem.at[1],
                    device_id=(lax.div(other, grid[1]), lax.rem(other, grid[1])),
                    device_id_type=MESH,
                ).start()

        return ready

    pick_nodes(
        grid, parts, [force[c] for c in range(3)], node_in, node_hot, back_f,
        sender(back_f, back_f_in, backf_sem),
    )
    back_f_in[me] = back_f[me]

    def back_row(a):
        return pltpu.roll(a, full[0] - 1, 0)

    def back_col(a):
        return pltpu.roll(a, full[1] - 1, 1)

    settle(grid, stat_strip, stat_sem.at[0], stat_sem.at[1])
    moduli = with_rim(stat, stat_strip, 0)
    live = with_rim(stat, stat_strip, 1)
    mass = with_rim(stat, stat_strip, 2)
    next_row = back_row(moduli)
    scale = live * (moduli + next_row + back_col(moduli) + back_col(next_row)) * 0.25

    def operate(fields):
        down = [back_row(f) for f in fields]
        corners = (
            list(fields) + down + [back_col(f) for f in fields] + [back_col(f) for f in down]
        )
        results = []
        for k in range(12):
            total = stiff[k, 0] * corners[0]
            for l in range(1, 12):
                total = total + stiff[k, l] * corners[l]
            results.append(scale * total)
        images = []
        for c in range(3):
            right = results[6 + c] + pltpu.roll(results[9 + c], 1, 0)
            images.append(
                mass * fields[c]
                + results[c]
                + pltpu.roll(results[3 + c], 1, 0)
                + pltpu.roll(right, 1, 1)
            )
        return images

    def inner(a, b):
        total = a[0] * b[0]
        for c in range(1, 3):
            total = total + a[c] * b[c]
        return jnp.sum(jnp.sum(total, axis=0, keepdims=True), axis=1, keepdims=True)

    settle(grid, strip, rim_sem.at[0], rim_sem.at[1])
    field = [with_rim(force, strip, c) for c in range(3)]
    image = operate(field)
    f = [a[:rows, :cols] for a in field]
    q = [a[:rows, :cols] for a in image]
    for c in range(3):
        image_buf[c] = q[c]
    pick_nodes(grid, parts, q, node_in, node_hot, back_q, sender(back_q, back_q_in, backq_sem))
    back_q_in[me] = back_q[me]
    second = operate(image)
    s = [a[:rows, :cols] for a in second]
    ff, fq, qq, qs = inner(f, f), inner(f, q), inner(q, q), inner(q, s)
    guess = jnp.where(qq > 0.0, fq / jnp.where(qq > 0.0, qq, 1.0), 0.0)
    r0 = [f[c] - guess * q[c] for c in range(3)]
    u0 = [q[c] - guess * s[c] for c in range(3)]
    mine = [
        ff, fq, qq, qs, guess, inner(r0, r0), inner(r0, q), inner(r0, u0), inner(r0, s), inner(q, u0)
    ]
    lane = iota((1, LANES), 1)
    line = jnp.zeros((1, LANES), F32)
    for k, value in enumerate(mine):
        line = jnp.where(lane == k, value, line)
    sums[me] = line
    send_all(
        grid, lambda o: sums.at[me], lambda m: sums.at[m], sum_sem.at[0], lambda j: sum_sem.at[1]
    )

    settle(grid, xu_in, lb_send.at[0], lb_recv.at[0])
    settle(grid, xd_in, lb_send.at[1], lb_recv.at[1])
    settle(grid, corner_in, lb_send.at[2], lb_recv.at[2])
    settle(grid, yu_in, lb_send.at[3], lb_recv.at[3])
    settle(grid, yd_in, lb_send.at[4], lb_recv.at[4])
    mend_edges(read, xu_in, xd_in, yu_in, yd_in, corner_in)
    settle(grid, sums.at[others], sum_sem.at[0], sum_sem.at[1])
    every = sums[...].reshape(devices, LANES)
    ff, fq, qq, qs, guess, r0r0, r0q, r0u0, r0s, qu0 = [
        every[:, k : k + 1] for k in range(len(mine))
    ]

    def total(value):
        return jnp.sum(value, axis=0, keepdims=True)

    ff_all, fq_all = total(ff), total(fq)
    first = ff_all / fq_all
    off = guess - first
    rr = total(r0r0 + off * (2.0 * r0q + off * qq))
    rs = total(r0u0 + off * (r0s + qu0 + off * qs))
    rq = total(r0q + off * qq)
    ratio = rr / ff_all
    step_two = rr / (rs + 2.0 * ratio * rq + ratio * ratio * fq_all)
    alpha = first + step_two * (1.0 + ratio)
    beta = -(step_two * first)
    scal_out[0:1] = jnp.broadcast_to(alpha, (1, LANES))
    scal_out[1:2] = jnp.broadcast_to(beta, (1, LANES))
    settle(grid, pay.at[others], pay_send.at[0], None)
    settle(grid, back_f_in.at[others], backf_sem.at[0], backf_sem.at[1])
    settle(grid, back_q_in.at[others], backq_sem.at[0], backq_sem.at[1])


def couple(grid, parts, stiff, populations, weights, blk, own, node, modulus, live, mass):
    devices = grid[0] * grid[1]
    _, nx, ny, nz = populations.shape
    records = weights.shape[0]
    patch = (3,) + mass.shape
    slots = parts * LANES
    vmem = pl.BlockSpec(memory_space=pltpu.VMEM)
    hbm = pl.BlockSpec(memory_space=pltpu.HBM)
    rim = [pltpu.VMEM((2, 3, 8, patch[2]), F32), pltpu.VMEM((8, 3, 8, patch[2]), F32)]
    pay = (devices, 3 * parts, LANES)
    back = jax.ShapeDtypeStruct(pay, F32)
    dma = pltpu.SemaphoreType.DMA
    lines = pltpu.VMEM((1, records), jnp.int32)
    edges = pltpu.VMEM((5, nx, 1, nz), F32)
    return pl.pallas_call(
        functools.partial(couple_kernel, grid, parts),
        in_specs=[hbm] * 9,
        out_specs=[vmem] * 10,
        out_shape=[
            jax.ShapeDtypeStruct(populations.shape, F32),
            jax.ShapeDtypeStruct((nz, records), F32),
            jax.ShapeDtypeStruct(patch, F32),
            jax.ShapeDtypeStruct(patch, F32),
            jax.ShapeDtypeStruct((1, records), jnp.int32),
            jax.ShapeDtypeStruct((2, LANES), F32),
            back,
            back,
            jax.ShapeDtypeStruct((1, records), jnp.int32),
            jax.ShapeDtypeStruct((1, records), jnp.int32),
        ],
        scratch_shapes=[
            pltpu.SMEM(stiff.shape, F32),
            pltpu.VMEM(populations.shape, F32),
            pltpu.VMEM((3, nx, ny, nz), F32),
            pltpu.VMEM((3 * nz, 2 * nx * ny), BF16),
            pltpu.VMEM(weights.shape, F32),
            lines,
            pltpu.VMEM((slots, records), BF16),
            pltpu.VMEM((8, records), F32),
            pltpu.VMEM((5, ny, nz), F32),
            pltpu.VMEM((5, ny, nz), F32),
            edges, edges, edges, edges,
            pltpu.VMEM((4, 1, nz), F32),
            pltpu.VMEM((devices, 1, slots), F32),
            pltpu.VMEM((devices, 1, slots), F32),
            pltpu.VMEM((devices, 2 * patch[2], slots), BF16),
            pltpu.VMEM(pay, F32),
            pltpu.VMEM(pay, F32),
            pltpu.VMEM(pay, F32),
            pltpu.VMEM(pay, F32),
            pltpu.VMEM(mass.shape, jnp.int32),
            pltpu.VMEM(patch, F32),
            *rim,
            *rim,
            pltpu.VMEM((devices, 1, LANES), F32),
            dma((4,)), dma((records // (4 * LANES),)), dma((7,)),
            dma((2,)), dma((1,)), dma((devices // math.gcd(devices, 8),)), dma((2,)), dma((2,)),
            dma((5,)), dma((5,)), dma((2,)), dma((2,)), dma((2,)),
        ],
        compiler_params=pltpu.CompilerParams(
            collective_id=0, has_side_effects=True, vmem_limit_bytes=36 * 2**20
        ),
        name="couple",
    )(stiff, populations, weights, blk, own, node, modulus, live, mass)


def finish_kernel(
    parts, scal, force, image, backf, backq, blk, own, slot, turned, read,
    out_hbm, disp_hbm,
    out, block_hot, forcing, moved, disp, out_sem,
):
    devices = backf.shape[0]
    depth, records = turned.shape
    _, nx, ny, nz = read.shape
    blocks = nx * ny
    slots = parts * LANES
    span = 4 * LANES
    steps = records // span
    stages = [
        [q for q in range(1, 19) if lattice_dirs[q][1] == 0 and lattice_dirs[q][2] == 0],
        [q for q in range(19) if lattice_dirs[q][1] != 0 and lattice_dirs[q][2] == 0],
        [q for q in range(19) if lattice_dirs[q][2] != 0],
    ]
    out_copies = [
        pltpu.make_async_copy(out.at[q], out_hbm.at[q], out_sem.at[q]) for q in range(19)
    ]
    alpha = scal[0:1]
    beta = scal[1:2]

    def rest_step(row, carry):
        out[0, row] = read[0, row]
        return carry

    lax.fori_loop(0, nx, rest_step, 0, unroll=4)
    out_copies[0].start()
    for c in range(3):
        disp[c] = alpha * force[c] + beta * image[c]
    disp_copy = pltpu.make_async_copy(disp, disp_hbm, out_sem.at[19])
    disp_copy.start()
    back = alpha.reshape(1, 1, LANES) * backf[...] + beta.reshape(1, 1, LANES) * backq[...]
    wide = jnp.concatenate([back[:, p * 3 : p * 3 + 3] for p in range(parts)], axis=2)
    high = wide.astype(BF16).astype(F32)
    left = jnp.concatenate([high, wide - high, jnp.zeros((devices, 2, slots), F32)], axis=1)
    left = left.reshape(devices * 8, slots).astype(BF16)

    def move_step(k, carry):
        at = pl.multiple_of(k * span, span)
        found = dot_nn(left, one_hot(slots, slot[:, pl.ds(at, span)]))
        owners = own[:, pl.ds(at, span)]
        lines = [jnp.zeros((8, span), F32) for _ in range(4)]
        for o in range(devices):
            lines[o % 4] = lines[o % 4] + jnp.where(owners == o, found[o * 8 : o * 8 + 8], 0.0)
        lines = (lines[0] + lines[1]) + (lines[2] + lines[3])
        value = coupling * (lines[:3] + lines[3:6])
        moved[:, pl.ds(at, span)] = jnp.concatenate([value, jnp.zeros((5, span), F32)], axis=0)
        block_hot[:, pl.ds(at, span)] = one_hot(blocks, blk[:, pl.ds(at, span)])
        return carry

    lax.fori_loop(0, steps, move_step, 0)
    for c in range(3):
        total = None
        for k in range(steps):
            at = k * span
            hot = block_hot[:, at : at + span]
            high, low = halves(turned[:, at : at + span] * moved[c : c + 1, at : at + span])
            part = dot_nt(jnp.concatenate([high, low], axis=0), hot)
            total = part if total is None else total + part
        forcing[c] = (total[:depth] + total[depth:]).T.reshape(nx, ny, nz)

        def row_step(row, carry, c=c):
            fields = [forcing[axis_pos, row] if axis_pos <= c else None for axis_pos in range(3)]
            for q in stages[c]:
                projected = combine_dirs(fields, lattice_dirs[q])
                out[q, row] = read[q, row] + (3.0 * lattice_weights[q]) * projected
            return carry

        lax.fori_loop(0, nx, row_step, 0, unroll=2)
        for q in stages[c]:
            out_copies[q].start()
    disp_copy.wait()
    for copy in out_copies:
        copy.wait()


def finish(parts, scal, force, image, back_f, back_q, blk, own, slot, turned, read):
    hbm = pl.BlockSpec(memory_space=pltpu.HBM)
    vmem = pl.BlockSpec(memory_space=pltpu.VMEM)
    records = blk.shape[1]
    dma = pltpu.SemaphoreType.DMA
    return pl.pallas_call(
        functools.partial(finish_kernel, parts),
        in_specs=[vmem] * 10,
        out_specs=[hbm, hbm],
        out_shape=[
            jax.ShapeDtypeStruct(read.shape, F32),
            jax.ShapeDtypeStruct(force.shape, F32),
        ],
        scratch_shapes=[
            pltpu.VMEM(read.shape, F32),
            pltpu.VMEM((read.shape[1] * read.shape[2], records), BF16),
            pltpu.VMEM((3,) + read.shape[1:], F32),
            pltpu.VMEM((8, records), F32),
            pltpu.VMEM(force.shape, F32),
            dma((20,)),
        ],
        compiler_params=pltpu.CompilerParams(vmem_limit_bytes=24 * 2**20),
        name="finish",
    )(scal, force, image, back_f, back_q, blk, own, slot, turned, read)


def per_device(
    grid, populations, mass, modulus, cell_live, stiff_ref, rec_block, rec_owner, rec_node,
    rbf_weight,
):
    devices = grid[0] * grid[1]
    records = rec_block.shape[0]
    capacity = 2 * records // devices
    parts = -(-capacity // LANES)
    blk = rec_block.reshape(1, records)
    own = rec_owner.reshape(1, records)
    node = rec_node.reshape(1, records)
    operands = [
        pltpu.with_memory_space_constraint(a, pltpu.HBM)
        for a in (stiff_ref, populations, rbf_weight, blk, own, node, modulus, cell_live, mass)
    ]
    read, turned, force, image, slot, scal, back_f, back_q, held_blk, held_own = couple(
        grid, parts, *operands
    )
    return finish(
        parts, scal, force, image, back_f, back_q, held_blk, held_own, slot, turned, read
    )


def solution(mesh):
    grid = (mesh.shape["gx"], mesh.shape["gy"])
    in_specs = (
        P(None, "gx", "gy", None),
        P("gx", "gy"),
        P("gx", "gy"),
        P("gx", "gy"),
        P(),
        P(("gx", "gy")),
        P(("gx", "gy"), None),
        P(("gx", "gy")),
        P(("gx", "gy"), None),
    )
    out_specs = (P(None, "gx", "gy", None), P(None, "gx", "gy"))
    return jax.shard_map(
        functools.partial(per_device, grid), mesh=mesh, in_specs=in_specs, out_specs=out_specs,
        check_vma=False,
    )
```

time: 59.4 us -> 46.7 us (0.79)
  Pallas kernels: 58.4 us -> 45.8 us
    pallas_call x2, Pallas kernels: 58.4 us -> 45.8 us  [the longest x1 34.9 us: couple(): pl.pallas_call(functools.partial(couple_kernel, grid, parts), in_specs=[h...]
where the time goes in v3:
time: 46.7 us; the launch traced here: 46.5 us
  Pallas kernels  45.8 us (98%)
  between operations  0.64 us (1%)
    pallas_call x1, Pallas kernels, couple(): pl.pallas_call(functools.partial(couple_kernel, grid, parts), in_specs=[h...  34.9 us
    pallas_call x1, Pallas kernels, finish(): pl.pallas_call(functools.partial(finish_kernel, parts), in_specs=[vmem] *...  10.9 us

profile of v3, /device:TPU:0, one launch (start us, length us, event | category | flops | bytes accessed | tf_op | source)
XLA Modules:
  0.0 46.5 jit_solution(2899087532584315123)
XLA Ops:
  0.6 34.9 %couple.1 = (f32[19,32,8,256]{3,2,1,0:T(8,128)S(1)}, f32[256,4096]{1,0:T(8,128)S(1)}, f32[3,64,128]{2,1,0:T(8,128)S(1)}, f32[3,64,128]{2,1,0:T(8,128)S(1)}, s32[...) custom-call(f32[12,12]{1,0:T(8,128)} %stiff_hbm.1, ...), custom_call_target="tpu_custom_call" | custom-call | tf_op jit(solution)/shard_map/couple/pallas_call | solution.py:690
  35.6 10.9 %finish.1 = (f32[19,32,8,256]{3,2,1,0:T(8,128)}, f32[3,64,128]{2,1,0:T(8,128)}) custom-call(f32[2,128]{1,0:T(2,128)S(1)} %get-tuple-element.12.scal, f32[3,64,128]{2,1,0:T(8,128)S(1)} %get-tuple-element.13.force, f32[3,64,128]{2,1,0:T(8,128)S(1)} %get-tuple-element.14.image, f32[32,6,128]{2,1,0:T(8,128)S(1)} %get-tuple-element.15.backf, ...), custom_call_target="tpu_custom_call" | custom-call | tf_op jit(solution)/shard_map/finish/pallas_call | solution.py:825

commit v4 on v3

--- a/solution.py
+++ b/solution.py
@@ -198,12 +198,17 @@
     return jnp.where(ramp == spread_rows(index, count), one, jnp.zeros(ramp.shape, BF16))
 
 
+def add_to(chains, number, part):
+    held = chains[number]
+    chains[number] = part if held is None else held + part
+
+
 def owner_mask(devices, owners):
     lines = (iota((devices * 8, owners.shape[1]), 0) // 8).astype(F32).astype(BF16)
     return lines == spread_rows(owners.astype(F32), devices * 8)
 
 
-def find_slots(devices, node_cols, own_ref, node_ref, slot_ref, slot_hot, node_pay):
+def find_slots(devices, node_cols, own_ref, node_ref, slot_hot, node_pay):
     records = own_ref.shape[1]
     slots = slot_hot.shape[0]
     span = 2 * LANES
@@ -216,7 +221,6 @@
         counts = dot_nn(hits, before)
         slot = jnp.sum(hits.astype(F32) * (counts + base), axis=0, keepdims=True)
         base = base + jnp.broadcast_to(counts[:, span - 1 :], (devices, span))
-        slot_ref[:, i * span : (i + 1) * span] = slot.astype(jnp.int32)
         hot = one_hot(slots, slot)
         slot_hot[:, i * span : (i + 1) * span] = hot
         node = node_ref[:, i * span : (i + 1) * span]
@@ -333,7 +337,7 @@
     rows, cols = force.shape[1:]
     half = rows // 2
     count = math.gcd(devices, 8)
-    total = None
+    chains = [None, None]
     for step in range(devices // count):
         arrived(step)
         for d in range(count):
@@ -347,11 +351,16 @@
                 high = value.astype(BF16).astype(F32)
                 highs.append(row_hot * spread_rows(high, half))
                 lows.append(row_hot * spread_rows(value - high, half))
-            part = dot_nt(jnp.concatenate(highs + lows, axis=0), node_hot[source])
-            total = part if total is None else total + part
-    total = total[: 3 * half] + total[3 * half :]
+            for number in range(2):
+                lines = slice(number * half // 2, (number + 1) * half // 2)
+                left = jnp.concatenate([piece[lines] for piece in highs + lows], axis=0)
+                add_to(chains, number, dot_nt(left, node_hot[source]))
+    middle = half // 2
+    chains = [chain[: 3 * middle] + chain[3 * middle :] for chain in chains]
     for c in range(3):
-        piece = total[c * half : (c + 1) * half]
+        piece = jnp.concatenate(
+            [chain[c * middle : (c + 1) * middle] for chain in chains], axis=0
+        )
         force[c] = jnp.concatenate([piece[:, :cols], piece[:, cols:]], axis=0)
 
 
@@ -391,8 +400,8 @@
 
 def couple_kernel(
     grid, parts, stiff_hbm, pop_hbm, w_hbm, blk_hbm, own_hbm, node_hbm, modulus_hbm, live_hbm, mass_hbm,
-    read, turned, force, image_buf, slot, scal_out, back_f_in, back_q_in, blk, own,
-    stiff, pop, mom, mom_cat, w, node, slot_hot, loads,
+    read, turned, force, image_buf, slot_hot, hot_turned, scal_out, back_f_in, back_q_in, own,
+    stiff, pop, mom, mom_cat, w, node, blk, loads,
     xu_in, xd_in, yu_out, yd_out, yu_in, yd_in, corner_in,
     node_pay, node_in, node_hot, pay, pay_in, back_f, back_q,
     live_in, stat, stat_out, stat_strip, side_out, strip, sums,
@@ -436,14 +445,15 @@
 
     for copy in small + pop_copies:
         copy.start()
-    for k in range(steps):
-        w_copy(k).start()
     for copy in small[:3]:
         copy.wait()
-    find_slots(devices, cols, own, node, slot, slot_hot, node_pay)
+    find_slots(devices, cols, own, node, slot_hot, node_pay)
 
     for k, copy in enumerate(pop_copies):
         copy.wait()
+        if k == 1:
+            for number in range(steps):
+                w_copy(number).start()
 
         def moment_row(row, carry):
             moments(pop, mom, row)
@@ -454,12 +464,18 @@
         high, low = halves(mom[c].reshape(blocks, nz).T)
         mom_cat[c * nz : (c + 1) * nz, :blocks] = high
         mom_cat[c * nz : (c + 1) * nz, blocks:] = low
+    for copy in small[3:]:
+        copy.wait()
+    stat[1] = live_in[...].astype(F32)
+    pack_side(stat, stat_out)
     await_all(grid)
     send_all(
         grid, lambda o: node_pay.at[o], lambda m: node_in.at[m], node_sem.at[0],
         lambda j: node_sem.at[1],
     )
     node_in[me] = node_pay[me]
+    for copy in rim_copies(grid, stat, stat_out, stat_strip, stat_sem.at[0], stat_sem.at[1]):
+        copy.start()
 
     def load_step(k, carry):
         w_copy(k).wait()
@@ -481,7 +497,7 @@
         return carry
 
     lax.fori_loop(0, steps, load_step, 0)
-    routed = None
+    chains = [None, None]
     for k in range(steps):
         at = k * span
         value = loads[:, at : at + span]
@@ -490,8 +506,10 @@
         spread = jnp.where(
             owner_mask(devices, own[:, at : at + span]), value, jnp.zeros(value.shape, BF16)
         )
-        part = dot_nt(spread, slot_hot[:, at : at + span])
-        routed = part if routed is None else routed + part
+        for number in range(2):
+            band = slice(number * devices * 4, (number + 1) * devices * 4)
+            add_to(chains, number, dot_nt(spread[band], slot_hot[:, at : at + span]))
+    routed = jnp.concatenate(chains, axis=0)
     for o in range(devices):
         tile = routed[o * 8 : o * 8 + 3] + routed[o * 8 + 3 : o * 8 + 6]
         pay[o] = jnp.concatenate(
@@ -503,12 +521,6 @@
         lambda j: pay_recv.at[lax.div(j, batch)],
     )
     pay_in[me] = pay[me]
-    for copy in small[3:]:
-        copy.wait()
-    stat[1] = live_in[...].astype(F32)
-    pack_side(stat, stat_out)
-    for copy in rim_copies(grid, stat, stat_out, stat_strip, stat_sem.at[0], stat_sem.at[1]):
-        copy.start()
 
     settle(grid, node_in.at[others], node_sem.at[0], node_sem.at[1])
 
@@ -647,6 +659,9 @@
     settle(grid, yu_in, lb_send.at[3], lb_recv.at[3])
     settle(grid, yd_in, lb_send.at[4], lb_recv.at[4])
     mend_edges(read, xu_in, xd_in, yu_in, yd_in, corner_in)
+    for k in range(steps):
+        hot = one_hot(blocks, blk[:, k * span : (k + 1) * span])
+        hot_turned[k * span : (k + 1) * span] = hot.T
     settle(grid, sums.at[others], sum_sem.at[0], sum_sem.at[1])
     every = sums[...].reshape(devices, LANES)
     ff, fq, qq, qs, guess, r0r0, r0q, r0u0, r0s, qu0 = [
@@ -696,11 +711,11 @@
             jax.ShapeDtypeStruct((nz, records), F32),
             jax.ShapeDtypeStruct(patch, F32),
             jax.ShapeDtypeStruct(patch, F32),
-            jax.ShapeDtypeStruct((1, records), jnp.int32),
+            jax.ShapeDtypeStruct((slots, records), BF16),
+            jax.ShapeDtypeStruct((records, nx * ny), BF16),
             jax.ShapeDtypeStruct((2, LANES), F32),
             back,
             back,
-            jax.ShapeDtypeStruct((1, records), jnp.int32),
             jax.ShapeDtypeStruct((1, records), jnp.int32),
         ],
         scratch_shapes=[
@@ -709,8 +724,7 @@
             pltpu.VMEM((3, nx, ny, nz), F32),
             pltpu.VMEM((3 * nz, 2 * nx * ny), BF16),
             pltpu.VMEM(weights.shape, F32),
-            lines,
-            pltpu.VMEM((slots, records), BF16),
+            lines, lines,
             pltpu.VMEM((8, records), F32),
             pltpu.VMEM((5, ny, nz), F32),
             pltpu.VMEM((5, ny, nz), F32),
@@ -740,9 +754,9 @@
 
 
 def finish_kernel(
-    parts, scal, force, image, backf, backq, blk, own, slot, turned, read,
+    parts, scal, force, image, backf, backq, own, slot_hot, hot_turned, turned, read,
     out_hbm, disp_hbm,
-    out, block_hot, forcing, moved, disp, out_sem,
+    out, forcing, moved, disp, out_sem,
 ):
     devices = backf.shape[0]
     depth, records = turned.shape
@@ -780,7 +794,7 @@
 
     def move_step(k, carry):
         at = pl.multiple_of(k * span, span)
-        found = dot_nn(left, one_hot(slots, slot[:, pl.ds(at, span)]))
+        found = dot_nn(left, slot_hot[:, pl.ds(at, span)])
         owners = own[:, pl.ds(at, span)]
         lines = [jnp.zeros((8, span), F32) for _ in range(4)]
         for o in range(devices):
@@ -788,19 +802,20 @@
         lines = (lines[0] + lines[1]) + (lines[2] + lines[3])
         value = coupling * (lines[:3] + lines[3:6])
         moved[:, pl.ds(at, span)] = jnp.concatenate([value, jnp.zeros((5, span), F32)], axis=0)
-        block_hot[:, pl.ds(at, span)] = one_hot(blocks, blk[:, pl.ds(at, span)])
         return carry
 
-    lax.fori_loop(0, steps, move_step, 0)
+    lax.fori_loop(0, steps, move_step, 0, unroll=2)
     for c in range(3):
-        total = None
+        chains = [None, None]
         for k in range(steps):
             at = k * span
-            hot = block_hot[:, at : at + span]
             high, low = halves(turned[:, at : at + span] * moved[c : c + 1, at : at + span])
-            part = dot_nt(jnp.concatenate([high, low], axis=0), hot)
-            total = part if total is None else total + part
-        forcing[c] = (total[:depth] + total[depth:]).T.reshape(nx, ny, nz)
+            for number in range(2):
+                band = slice(number * depth // 2, (number + 1) * depth // 2)
+                left = jnp.concatenate([high[band], low[band]], axis=0)
+                add_to(chains, number, dot_nn(left, hot_turned[at : at + span]))
+        chains = [chain[: depth // 2] + chain[depth // 2 :] for chain in chains]
+        forcing[c] = jnp.concatenate(chains, axis=0).T.reshape(nx, ny, nz)
 
         def row_step(row, carry, c=c):
             fields = [forcing[axis_pos, row] if axis_pos <= c else None for axis_pos in range(3)]
@@ -817,10 +832,10 @@
         copy.wait()
 
 
-def finish(parts, scal, force, image, back_f, back_q, blk, own, slot, turned, read):
+def finish(parts, scal, force, image, back_f, back_q, own, slot_hot, hot_turned, turned, read):
     hbm = pl.BlockSpec(memory_space=pltpu.HBM)
     vmem = pl.BlockSpec(memory_space=pltpu.VMEM)
-    records = blk.shape[1]
+    records = own.shape[1]
     dma = pltpu.SemaphoreType.DMA
     return pl.pallas_call(
         functools.partial(finish_kernel, parts),
@@ -832,7 +847,6 @@
         ],
         scratch_shapes=[
             pltpu.VMEM(read.shape, F32),
-            pltpu.VMEM((read.shape[1] * read.shape[2], records), BF16),
             pltpu.VMEM((3,) + read.shape[1:], F32),
             pltpu.VMEM((8, records), F32),
             pltpu.VMEM(force.shape, F32),
@@ -840,7 +854,7 @@
         ],
         compiler_params=pltpu.CompilerParams(vmem_limit_bytes=24 * 2**20),
         name="finish",
-    )(scal, force, image, back_f, back_q, blk, own, slot, turned, read)
+    )(scal, force, image, back_f, back_q, own, slot_hot, hot_turned, turned, read)
 
 
 def per_device(
@@ -858,11 +872,11 @@
         pltpu.with_memory_space_constraint(a, pltpu.HBM)
         for a in (stiff_ref, populations, rbf_weight, blk, own, node, modulus, cell_live, mass)
     ]
-    read, turned, force, image, slot, scal, back_f, back_q, held_blk, held_own = couple(
+    read, turned, force, image, slot_hot, hot_turned, scal, back_f, back_q, held_own = couple(
         grid, parts, *operands
     )
     return finish(
-        parts, scal, force, image, back_f, back_q, held_blk, held_own, slot, turned, read
+        parts, scal, force, image, back_f, back_q, held_own, slot_hot, hot_turned, turned, read
     )
 
 

time: 46.7 us -> 44 us (0.942)
  Pallas kernels: 45.8 us -> 43.1 us
    pallas_call x1, Pallas kernels: 10.9 us -> 8.12 us  [finish(): pl.pallas_call(functools.partial(finish_kernel, parts), in_specs=[vmem] *...]
where the time goes in v4:
time: 44 us; the launch traced here: 43.7 us
  Pallas kernels  43.1 us (98%)
  between operations  0.64 us (1%)
    pallas_call x1, Pallas kernels, couple(): pl.pallas_call(functools.partial(couple_kernel, grid, parts), in_specs=[h...  35 us
    pallas_call x1, Pallas kernels, finish(): pl.pallas_call(functools.partial(finish_kernel, parts), in_specs=[vmem] *...  8.12 us

profile of v4, /device:TPU:0, one launch (start us, length us, event | category | flops | bytes accessed | tf_op | source)
XLA Modules:
  0.0 43.7 jit_solution(13872142199993948376)
XLA Ops:
  0.6 35.0 %couple.1 = (f32[19,32,8,256]{3,2,1,0:T(8,128)S(1)}, f32[256,4096]{1,0:T(8,128)S(1)}, f32[3,64,128]{2,1,0:T(8,128)S(1)}, f32[3,64,128]{2,1,0:T(8,128)S(1)}, bf16...) custom-call(f32[12,12]{1,0:T(8,128)} %stiff_hbm.1, ...), custom_call_target="tpu_custom_call" | custom-call | tf_op jit(solution)/shard_map/couple/pallas_call | solution.py:705
  35.6 8.1 %finish.1 = (f32[19,32,8,256]{3,2,1,0:T(8,128)}, f32[3,64,128]{2,1,0:T(8,128)}) custom-call(f32[2,128]{1,0:T(2,128)S(1)} %get-tuple-element.12.scal, f32[3,64,128]{2,1,0:T(8,128)S(1)} %get-tuple-element.13.force, f32[3,64,128]{2,1,0:T(8,128)S(1)} %get-tuple-element.14.image, f32[32,6,128]{2,1,0:T(8,128)S(1)} %get-tuple-element.15.backf, ...), custom_call_target="tpu_custom_call" | custom-call | tf_op jit(solution)/shard_map/finish/pallas_call | solution.py:840

commit v5 on v4

--- a/solution.py
+++ b/solution.py
@@ -79,21 +79,34 @@
     return lax.axis_index("gx"), lax.axis_index("gy")
 
 
+def each_other(devices, body):
+    batch = 6
+    rounds = (devices - 1) // batch
+
+    def one(step, carry):
+        for d in range(batch):
+            body(step * batch + d + 1)
+        return carry
+
+    lax.fori_loop(0, rounds, one, 0)
+    for j in range(rounds * batch + 1, devices):
+        body(j)
+
+
 def greet_all(grid):
     ix, iy = position(grid)
     devices = grid[0] * grid[1]
     me = ix * grid[1] + iy
     barrier = pltpu.get_barrier_semaphore()
 
-    def signal(j, carry):
+    def signal(j):
         other = lax.rem(me + j, devices)
         pl.semaphore_signal(
             barrier, inc=1, device_id=(lax.div(other, grid[1]), lax.rem(other, grid[1])),
             device_id_type=MESH,
         )
-        return carry
-
-    lax.fori_loop(1, devices, signal, 0)
+
+    each_other(devices, signal)
 
 
 def await_all(grid):
@@ -105,7 +118,7 @@
     devices = grid[0] * grid[1]
     me = ix * grid[1] + iy
 
-    def body(j, carry):
+    def body(j):
         other = lax.rem(me + j, devices)
         pltpu.make_async_remote_copy(
             src_ref=source(other),
@@ -115,9 +128,8 @@
             device_id=(lax.div(other, grid[1]), lax.rem(other, grid[1])),
             device_id_type=MESH,
         ).start()
-        return carry
-
-    lax.fori_loop(1, devices, body, 0)
+
+    each_other(devices, body)
 
 
 def neighbour_copy(grid, dx, dy, source, target, send_sem, recv_sem):
@@ -559,8 +571,11 @@
         settle(grid, pay_in.at[pl.ds(0, got)], None, pay_recv.at[step])
 
     gather_force(grid, parts, node_in, node_hot, pay_in, force, pay_arrived)
+    copies = rim_copies(grid, force, side_out, strip, rim_sem.at[0], rim_sem.at[1])
+    for copy in copies[:6]:
+        copy.start()
     pack_side(force, side_out)
-    for copy in rim_copies(grid, force, side_out, strip, rim_sem.at[0], rim_sem.at[1]) + lb_copies:
+    for copy in copies[6:] + lb_copies:
         copy.start()
 
     def sender(back, back_in, sem):
@@ -795,11 +810,15 @@
     def move_step(k, carry):
         at = pl.multiple_of(k * span, span)
         found = dot_nn(left, slot_hot[:, pl.ds(at, span)])
-        owners = own[:, pl.ds(at, span)]
-        lines = [jnp.zeros((8, span), F32) for _ in range(4)]
-        for o in range(devices):
-            lines[o % 4] = lines[o % 4] + jnp.where(owners == o, found[o * 8 : o * 8 + 8], 0.0)
-        lines = (lines[0] + lines[1]) + (lines[2] + lines[3])
+        found = jnp.where(
+            owner_mask(devices, own[:, pl.ds(at, span)]), found.astype(BF16),
+            jnp.zeros(found.shape, BF16),
+        )
+        lines = found[:16]
+        for o in range(1, devices // 2):
+            lines = lines + found[o * 16 : (o + 1) * 16]
+        lines = lines.astype(F32)
+        lines = lines[:8] + lines[8:]
         value = coupling * (lines[:3] + lines[3:6])
         moved[:, pl.ds(at, span)] = jnp.concatenate([value, jnp.zeros((5, span), F32)], axis=0)
         return carry

time: 44 us -> 43.5 us (0.989)
  Pallas kernels: 43.1 us -> 42.6 us
where the time goes in v5:
time: 43.5 us; the launch traced here: 43.3 us
  Pallas kernels  42.6 us (98%)
  between operations  0.64 us (1%)
    pallas_call x1, Pallas kernels, couple(): pl.pallas_call(functools.partial(couple_kernel, grid, parts), in_specs=[h...  34.6 us
    pallas_call x1, Pallas kernels, finish(): pl.pallas_call(functools.partial(finish_kernel, parts), in_specs=[vmem] *...  8.03 us

profile of v5, /device:TPU:0, one launch (start us, length us, event | category | flops | bytes accessed | tf_op | source)
XLA Modules:
  0.0 43.3 jit_solution(11383067501287891486)
XLA Ops:
  0.6 34.6 %couple.1 = (f32[19,32,8,256]{3,2,1,0:T(8,128)S(1)}, f32[256,4096]{1,0:T(8,128)S(1)}, f32[3,64,128]{2,1,0:T(8,128)S(1)}, f32[3,64,128]{2,1,0:T(8,128)S(1)}, bf16...) custom-call(f32[12,12]{1,0:T(8,128)} %stiff_hbm.1, ...), custom_call_target="tpu_custom_call" | custom-call | tf_op jit(solution)/shard_map/couple/pallas_call | solution.py:720
  35.3 8.0 %finish.1 = (f32[19,32,8,256]{3,2,1,0:T(8,128)}, f32[3,64,128]{2,1,0:T(8,128)}) custom-call(f32[2,128]{1,0:T(2,128)S(1)} %get-tuple-element.12.scal, f32[3,64,128]{2,1,0:T(8,128)S(1)} %get-tuple-element.13.force, f32[3,64,128]{2,1,0:T(8,128)S(1)} %get-tuple-element.14.image, f32[32,6,128]{2,1,0:T(8,128)S(1)} %get-tuple-element.15.backf, ...), custom_call_target="tpu_custom_call" | custom-call | tf_op jit(solution)/shard_map/finish/pallas_call | solution.py:859
